TPU v7x, 512 devices: a 4x2x32 block of a 4x8x32 slice. The times are simulated.
512 devices in a mesh: grp: 2 (over y), band: 32 (over z), mem: 4 (over x), fld: 2 (over core).
Axes of the slice: x: 4, y: 2, z: 32, core: 2. Of those that a mesh axis runs over, the one named last changes fastest.
The devices are a block of a 4x8x32 slice.
Arguments:
- surface_fields: bfloat16 [16, 8, 8, 524288], P(('grp', 'mem'), 'fld', None, 'band'), parts along dimension 0, may hold values from -8 to 8
- land_mask: int32 [524288], P('band'), may hold values from 0 to 1, as said below
- source_area: float32 [524288], P('band'), may hold values from 0.5 to 1.5
- target_area: float32 [131072], P('band'), may hold values from 0.75 to 1.25
- weight_tiles: bfloat16 [16, 128, 128], replicated, may hold values from -1 to 1
- tile_of: int32 [1024, 24], P('band'), may hold values from 0 to 15
- block_of: int32 [1024, 24], P('band'), may hold values from 0 to 191, as said below
- live_slots: int32 [1024], P('band'), may hold values from 1 to 24, as said below
Outputs:
- regridded: float32 [16, 8, 8, 131072], P(('grp', 'mem'), 'fld', None, 'band'), parts along dimension 0
- conserved: float32 [16, 8, 8], P(('grp', 'mem'), 'fld'), parts along dimension 0
- ensemble: float32 [16, 8], P(('grp', 'fld')), parts along dimension 0
There are 2 independent parts, one for each index of `grp`. A program takes and returns all parts, laid end to end along the dimension named above; an argument that names none is the same for every part. Nothing has to cross between parts.
Inputs may be any that keep to these rules, and one draw needn't show every extreme that they name: `land_mask`: 1 marks ocean, 0 land. `block_of`: for the target block at place j (0 to 31) within its band, every entry lies in 4 * j to 4 * j + 4 + 2 * 32 - 1; values under 32 name the lower band's last blocks, values from 160 on the higher band's first blocks. `live_slots`: slots from this count on are unused.
All inputs are finite; a program needn't handle non-finite values.
Results may differ from a plain program's by a relative error of at most 0.0014.
Values may be sent and summed in bfloat16 or wider, within the bound.
A program may use at most 64 MiB of HBM per device.

v0:
```python
import jax
import jax.numpy as jnp
from jax import lax
from jax.sharding import PartitionSpec as P

MEMBERS = 8
HALO_BLK = 32


def from_everyone(array, axis):
    length = lax.axis_size(axis)
    return lax.all_to_all(
        jnp.broadcast_to(array[None], (length, *array.shape)), axis, 0, 0, tiled=True
    )


def over_copies(array, axis):
    return from_everyone(array, axis).sum(axis=0)


def packed_total(arrays, axis):
    vector, at, gathered = (jnp.concatenate([a.reshape(-1) for a in arrays]), 0, [])
    subtotal = over_copies(vector, axis)
    for a in arrays:
        gathered.append(subtotal[at : at + a.size].reshape(a.shape))
        at += a.size
    return tuple(gathered)


def extended_2(array, sides, width):
    for axis, dim in sides:
        size, length = (lax.axis_size(axis), array.shape[dim])
        up = [(i, (i + 1) % size) for i in range(size - 1)]
        down = [(j, i) for i, j in up]
        last = lax.slice_in_dim(array, length - width, length, axis=dim)
        leading = lax.slice_in_dim(array, 0, width, axis=dim)
        before = lax.ppermute(last, axis, up)
        after = lax.ppermute(leading, axis, down)
        array = jnp.concatenate([before, array, after], axis=dim)
    return array


def slot_terms(source, slot_names, weight_tiles, bounds):
    tile_ids, picked, usable, unused = slot_names
    columns = source.shape[0]
    tile_size = source.shape[2]
    tgt_count = picked.shape[0]

    def one_slot(position, running):
        chosen = jnp.take(source, picked[:, position], axis=1)
        weights = jnp.take(weight_tiles, tile_ids[:, position], axis=0)
        weights = jnp.where(
            usable[:, position][:, None, None], weights, jnp.zeros((), weight_tiles.dtype)
        )
        return running + jnp.einsum(
            "cnb,nbd->cnd", chosen, weights, preferred_element_type=jnp.float32
        )

    start = jnp.zeros((columns, tgt_count, tile_size), jnp.float32)
    return lax.fori_loop(bounds[0], bounds[1], one_slot, start)


def band_totals(own_total, target_part, area_part):
    return packed_total((own_total, target_part, area_part), "band")


def on_device(
    surface_fields, land_mask, source_area, target_area, weight_tiles, tile_of, block_of, live_slots
):
    members, fields, snapshots, cell_count = surface_fields.shape
    columns = members * fields * snapshots
    tile_size = weight_tiles.shape[1]
    slot_count = tile_of.shape[1]
    tgt_count = tile_of.shape[0]
    own_blocks = cell_count // tile_size
    weighted = (
        source_area * land_mask.astype(jnp.float32) * surface_fields.astype(jnp.float32)
    ).astype(jnp.bfloat16)
    flat = weighted.reshape(columns, cell_count)
    own_total = jnp.sum(flat, axis=1, dtype=jnp.float32)
    area_part = jnp.sum(target_area)
    slot_place = lax.broadcasted_iota(jnp.int32, (tgt_count, slot_count), 1)
    slot_alive = slot_place < live_slots[:, None]

    def limits(counts):
        return (jnp.int32(0), jnp.max(counts))

    extended = extended_2(flat, (("band", 1),), HALO_BLK * tile_size)
    source = extended.reshape(columns, own_blocks + 2 * HALO_BLK, tile_size)
    work_list = [(tile_of, block_of, slot_alive, live_slots)]
    results = [slot_terms(source, listed, weight_tiles, limits(listed[3])) for listed in work_list]
    raw_sums = results[0]
    raw_sums = raw_sums.reshape(columns, tgt_count * tile_size)
    totals = band_totals(own_total, jnp.sum(raw_sums, axis=1), area_part)
    source_total, target_total, area_total = totals
    correction = (source_total - target_total) / area_total
    regridded = raw_sums / target_area[None, :] + correction[:, None]
    conserved = (source_total / area_total).reshape(members, fields, snapshots)
    ensemble = over_copies(jnp.sum(conserved, axis=0), "mem") / MEMBERS
    return (
        regridded.reshape(members, fields, snapshots, tgt_count * tile_size),
        conserved,
        ensemble,
    )


def solution(mesh):
    placed = (
        P(("grp", "mem"), "fld", None, "band"),
        P("band"),
        P("band"),
        P("band"),
        P(),
        P("band", None),
        P("band", None),
        P("band"),
    )
    return jax.shard_map(
        on_device,
        mesh=mesh,
        in_specs=placed,
        out_specs=(
            P(("grp", "mem"), "fld", None, "band"),
            P(("grp", "mem"), "fld", None),
            P(("grp", "fld"), None),
        ),
        check_vma=False,
    )
```

profile of v0, /device:TPU:40, one launch (start us, length us, event | category | flops | bytes accessed | tf_op | source)
XLA Modules:
  0.0 238.5 jit_solution(7671538234315292339)
XLA Ops:
  0.6 0.9 convert_multiply_fusion
  1.5 2.3 convert_reduce_fusion
  3.9 1.0 fusion.13
  4.9 4.7 %collective-permute-start = (bf16[64,4096]{1,0:T(8,128)(2,1)}, bf16[64,4096]{1,0:T(8,128)(2,1)S(1)}, u32[]{:S(2)}, u32[]{:S(2)}) collective-permute-start(bf16[64,4096]{1,0:T(8,128)(2,1)} %get-tuple-element.95), channel_id=1, source_target_pairs={{0,8},{8,16},{16,24},{24,32},{32,40},{40,48},{48,56},{56,64},{64,7... | collective-permute-start | bytes 1572872 | tf_op jit(solution)/shard_map/ppermute | solution.py:37
  9.7 1.3 collective-permute-start.1
  12.3 8.9 %collective-permute-done = bf16[64,4096]{1,0:T(8,128)(2,1)S(1)} collective-permute-done((bf16[64,4096]{1,0:T(8,128)(2,1)}, bf16[64,4096]{1,0:T(8,128)(2,1)S(1)}, u32[]{:S(2)}, u32[]{:S(2)}) %collective-permute-start) | collective-permute-done | bytes 524320 | tf_op jit(solution)/shard_map/ppermute | solution.py:37
  21.2 5.2 %collective-permute-done.1 = bf16[64,4096]{1,0:T(8,128)(2,1)} collective-permute-done((bf16[64,4096]{1,0:T(8,128)(2,1)}, bf16[64,4096]{1,0:T(8,128)(2,1)}, u32[]{:S(2)}, u32[]{:S(2)}) %collective-permute-start.1) | collective-permute-done | bytes 524320 | tf_op jit(solution)/shard_map/ppermute | solution.py:38
  26.4 3.0 %copy_bitcast_fusion = bf16[64,192,128]{2,0,1:T(8,128)(2,1)} fusion(bf16[64,4096]{1,0:T(8,128)(2,1)} %collective-permute-done.1, bf16[64,16384]{1,0:T(8,128)(2,1)S(1)} %bitcast.36, bf16[64,4096]{1,0:T(8,128)(2,1)S(1)} %collective-permute-done), kind=kLoop, calls=%fused_computation.27 | loop fusion | flops 9437184 | bytes 6291456 | tf_op jit(solution)/shard_map/while | solution.py:60
  29.4 130.8 %while.10 = (s32[]{:T(128)}, f32[64,32,128]{2,0,1:T(8,128)S(1)}, s32[]{:T(128)}, pred[32,24]{0,1:T(8,128)(4,1)S(1)}, s32[32,24]{0,1:T(8,128)}, /*index=5*/bf16[1...) while((s32[]{:T(128)}, f32[64,32,128]{2,0,1:T(8,128)S(1)}, ...), condition=%wide.region_2.0_spmd, body=%wide.region_1.0_spmd.sunk | while | flops 68684160 | bytes 6825335 | solution.py:60
  30.1 0.7 and_bitcast_fusion.3
  30.8 0.7 gather_fusion
  31.6 2.5 %gather_fusion.1 = bf16[32,64,128]{2,1,0:T(8,128)(2,1)S(1)} fusion(bf16[64,192,128]{2,0,1:T(8,128)(2,1)} %get-tuple-element.186, s32[1024]{0:T(1024)S(1)} %pad_clamp_fusion.5), kind=kCustom, calls=%fused_computation.1.clone.1 | custom fusion | bytes 1048704 | tf_op jit(solution)/shard_map/while/body/jit(_take)/gather | solution.py:50
  35.5 0.7 and_bitcast_fusion.3
  36.3 0.7 gather_fusion
  37.0 2.5 %gather_fusion.1 = bf16[32,64,128]{2,1,0:T(8,128)(2,1)S(1)} fusion(bf16[64,192,128]{2,0,1:T(8,128)(2,1)} %get-tuple-element.186, s32[1024]{0:T(1024)S(1)} %pad_clamp_fusion.5), kind=kCustom, calls=%fused_computation.1.clone.1 | custom fusion | bytes 1048704 | tf_op jit(solution)/shard_map/while/body/jit(_take)/gather | solution.py:50
  41.7 0.7 gather_fusion
  42.5 2.5 %gather_fusion.1 = bf16[32,64,128]{2,1,0:T(8,128)(2,1)S(1)} fusion(bf16[64,192,128]{2,0,1:T(8,128)(2,1)} %get-tuple-element.186, s32[1024]{0:T(1024)S(1)} %pad_clamp_fusion.5), kind=kCustom, calls=%fused_computation.1.clone.1 | custom fusion | bytes 1048704 | tf_op jit(solution)/shard_map/while/body/jit(_take)/gather | solution.py:50
  47.1 0.7 gather_fusion
  47.9 2.5 %gather_fusion.1 = bf16[32,64,128]{2,1,0:T(8,128)(2,1)S(1)} fusion(bf16[64,192,128]{2,0,1:T(8,128)(2,1)} %get-tuple-element.186, s32[1024]{0:T(1024)S(1)} %pad_clamp_fusion.5), kind=kCustom, calls=%fused_computation.1.clone.1 | custom fusion | bytes 1048704 | tf_op jit(solution)/shard_map/while/body/jit(_take)/gather | solution.py:50
  52.5 0.7 gather_fusion
  53.3 2.5 %gather_fusion.1 = bf16[32,64,128]{2,1,0:T(8,128)(2,1)S(1)} fusion(bf16[64,192,128]{2,0,1:T(8,128)(2,1)} %get-tuple-element.186, s32[1024]{0:T(1024)S(1)} %pad_clamp_fusion.5), kind=kCustom, calls=%fused_computation.1.clone.1 | custom fusion | bytes 1048704 | tf_op jit(solution)/shard_map/while/body/jit(_take)/gather | solution.py:50
  58.0 0.7 gather_fusion
  58.7 2.5 %gather_fusion.1 = bf16[32,64,128]{2,1,0:T(8,128)(2,1)S(1)} fusion(bf16[64,192,128]{2,0,1:T(8,128)(2,1)} %get-tuple-element.186, s32[1024]{0:T(1024)S(1)} %pad_clamp_fusion.5), kind=kCustom, calls=%fused_computation.1.clone.1 | custom fusion | bytes 1048704 | tf_op jit(solution)/shard_map/while/body/jit(_take)/gather | solution.py:50
  63.4 0.7 gather_fusion
  64.1 2.5 %gather_fusion.1 = bf16[32,64,128]{2,1,0:T(8,128)(2,1)S(1)} fusion(bf16[64,192,128]{2,0,1:T(8,128)(2,1)} %get-tuple-element.186, s32[1024]{0:T(1024)S(1)} %pad_clamp_fusion.5), kind=kCustom, calls=%fused_computation.1.clone.1 | custom fusion | bytes 1048704 | tf_op jit(solution)/shard_map/while/body/jit(_take)/gather | solution.py:50
  68.8 0.7 gather_fusion
  69.6 2.5 %gather_fusion.1 = bf16[32,64,128]{2,1,0:T(8,128)(2,1)S(1)} fusion(bf16[64,192,128]{2,0,1:T(8,128)(2,1)} %get-tuple-element.186, s32[1024]{0:T(1024)S(1)} %pad_clamp_fusion.5), kind=kCustom, calls=%fused_computation.1.clone.1 | custom fusion | bytes 1048704 | tf_op jit(solution)/shard_map/while/body/jit(_take)/gather | solution.py:50
  74.2 0.7 gather_fusion
  75.0 2.5 %gather_fusion.1 = bf16[32,64,128]{2,1,0:T(8,128)(2,1)S(1)} fusion(bf16[64,192,128]{2,0,1:T(8,128)(2,1)} %get-tuple-element.186, s32[1024]{0:T(1024)S(1)} %pad_clamp_fusion.5), kind=kCustom, calls=%fused_computation.1.clone.1 | custom fusion | bytes 1048704 | tf_op jit(solution)/shard_map/while/body/jit(_take)/gather | solution.py:50
  79.6 0.7 gather_fusion
  80.4 2.5 %gather_fusion.1 = bf16[32,64,128]{2,1,0:T(8,128)(2,1)S(1)} fusion(bf16[64,192,128]{2,0,1:T(8,128)(2,1)} %get-tuple-element.186, s32[1024]{0:T(1024)S(1)} %pad_clamp_fusion.5), kind=kCustom, calls=%fused_computation.1.clone.1 | custom fusion | bytes 1048704 | tf_op jit(solution)/shard_map/while/body/jit(_take)/gather | solution.py:50
  85.1 0.7 gather_fusion
  85.8 2.5 %gather_fusion.1 = bf16[32,64,128]{2,1,0:T(8,128)(2,1)S(1)} fusion(bf16[64,192,128]{2,0,1:T(8,128)(2,1)} %get-tuple-element.186, s32[1024]{0:T(1024)S(1)} %pad_clamp_fusion.5), kind=kCustom, calls=%fused_computation.1.clone.1 | custom fusion | bytes 1048704 | tf_op jit(solution)/shard_map/while/body/jit(_take)/gather | solution.py:50
  90.5 0.7 gather_fusion
  91.3 2.5 %gather_fusion.1 = bf16[32,64,128]{2,1,0:T(8,128)(2,1)S(1)} fusion(bf16[64,192,128]{2,0,1:T(8,128)(2,1)} %get-tuple-element.186, s32[1024]{0:T(1024)S(1)} %pad_clamp_fusion.5), kind=kCustom, calls=%fused_computation.1.clone.1 | custom fusion | bytes 1048704 | tf_op jit(solution)/shard_map/while/body/jit(_take)/gather | solution.py:50
  95.9 0.7 gather_fusion
  96.7 2.5 %gather_fusion.1 = bf16[32,64,128]{2,1,0:T(8,128)(2,1)S(1)} fusion(bf16[64,192,128]{2,0,1:T(8,128)(2,1)} %get-tuple-element.186, s32[1024]{0:T(1024)S(1)} %pad_clamp_fusion.5), kind=kCustom, calls=%fused_computation.1.clone.1 | custom fusion | bytes 1048704 | tf_op jit(solution)/shard_map/while/body/jit(_take)/gather | solution.py:50
  101.3 0.7 gather_fusion
  102.1 2.5 %gather_fusion.1 = bf16[32,64,128]{2,1,0:T(8,128)(2,1)S(1)} fusion(bf16[64,192,128]{2,0,1:T(8,128)(2,1)} %get-tuple-element.186, s32[1024]{0:T(1024)S(1)} %pad_clamp_fusion.5), kind=kCustom, calls=%fused_computation.1.clone.1 | custom fusion | bytes 1048704 | tf_op jit(solution)/shard_map/while/body/jit(_take)/gather | solution.py:50
  106.8 0.7 gather_fusion
  107.5 2.5 %gather_fusion.1 = bf16[32,64,128]{2,1,0:T(8,128)(2,1)S(1)} fusion(bf16[64,192,128]{2,0,1:T(8,128)(2,1)} %get-tuple-element.186, s32[1024]{0:T(1024)S(1)} %pad_clamp_fusion.5), kind=kCustom, calls=%fused_computation.1.clone.1 | custom fusion | bytes 1048704 | tf_op jit(solution)/shard_map/while/body/jit(_take)/gather | solution.py:50
  112.2 0.7 gather_fusion
  113.0 2.5 %gather_fusion.1 = bf16[32,64,128]{2,1,0:T(8,128)(2,1)S(1)} fusion(bf16[64,192,128]{2,0,1:T(8,128)(2,1)} %get-tuple-element.186, s32[1024]{0:T(1024)S(1)} %pad_clamp_fusion.5), kind=kCustom, calls=%fused_computation.1.clone.1 | custom fusion | bytes 1048704 | tf_op jit(solution)/shard_map/while/body/jit(_take)/gather | solution.py:50
  117.6 0.7 gather_fusion
  118.4 2.5 %gather_fusion.1 = bf16[32,64,128]{2,1,0:T(8,128)(2,1)S(1)} fusion(bf16[64,192,128]{2,0,1:T(8,128)(2,1)} %get-tuple-element.186, s32[1024]{0:T(1024)S(1)} %pad_clamp_fusion.5), kind=kCustom, calls=%fused_computation.1.clone.1 | custom fusion | bytes 1048704 | tf_op jit(solution)/shard_map/while/body/jit(_take)/gather | solution.py:50
  123.0 0.7 gather_fusion
  123.8 2.5 %gather_fusion.1 = bf16[32,64,128]{2,1,0:T(8,128)(2,1)S(1)} fusion(bf16[64,192,128]{2,0,1:T(8,128)(2,1)} %get-tuple-element.186, s32[1024]{0:T(1024)S(1)} %pad_clamp_fusion.5), kind=kCustom, calls=%fused_computation.1.clone.1 | custom fusion | bytes 1048704 | tf_op jit(solution)/shard_map/while/body/jit(_take)/gather | solution.py:50
  128.5 0.7 gather_fusion
  129.2 2.5 %gather_fusion.1 = bf16[32,64,128]{2,1,0:T(8,128)(2,1)S(1)} fusion(bf16[64,192,128]{2,0,1:T(8,128)(2,1)} %get-tuple-element.186, s32[1024]{0:T(1024)S(1)} %pad_clamp_fusion.5), kind=kCustom, calls=%fused_computation.1.clone.1 | custom fusion | bytes 1048704 | tf_op jit(solution)/shard_map/while/body/jit(_take)/gather | solution.py:50
  133.9 0.7 gather_fusion
  134.6 2.5 %gather_fusion.1 = bf16[32,64,128]{2,1,0:T(8,128)(2,1)S(1)} fusion(bf16[64,192,128]{2,0,1:T(8,128)(2,1)} %get-tuple-element.186, s32[1024]{0:T(1024)S(1)} %pad_clamp_fusion.5), kind=kCustom, calls=%fused_computation.1.clone.1 | custom fusion | bytes 1048704 | tf_op jit(solution)/shard_map/while/body/jit(_take)/gather | solution.py:50
  139.3 0.7 gather_fusion
  140.1 2.5 %gather_fusion.1 = bf16[32,64,128]{2,1,0:T(8,128)(2,1)S(1)} fusion(bf16[64,192,128]{2,0,1:T(8,128)(2,1)} %get-tuple-element.186, s32[1024]{0:T(1024)S(1)} %pad_clamp_fusion.5), kind=kCustom, calls=%fused_computation.1.clone.1 | custom fusion | bytes 1048704 | tf_op jit(solution)/shard_map/while/body/jit(_take)/gather | solution.py:50
  144.7 0.7 gather_fusion
  145.5 2.5 %gather_fusion.1 = bf16[32,64,128]{2,1,0:T(8,128)(2,1)S(1)} fusion(bf16[64,192,128]{2,0,1:T(8,128)(2,1)} %get-tuple-element.186, s32[1024]{0:T(1024)S(1)} %pad_clamp_fusion.5), kind=kCustom, calls=%fused_computation.1.clone.1 | custom fusion | bytes 1048704 | tf_op jit(solution)/shard_map/while/body/jit(_take)/gather | solution.py:50
  150.1 0.7 gather_fusion
  150.9 2.5 %gather_fusion.1 = bf16[32,64,128]{2,1,0:T(8,128)(2,1)S(1)} fusion(bf16[64,192,128]{2,0,1:T(8,128)(2,1)} %get-tuple-element.186, s32[1024]{0:T(1024)S(1)} %pad_clamp_fusion.5), kind=kCustom, calls=%fused_computation.1.clone.1 | custom fusion | bytes 1048704 | tf_op jit(solution)/shard_map/while/body/jit(_take)/gather | solution.py:50
  155.6 0.7 gather_fusion
  156.3 2.5 %gather_fusion.1 = bf16[32,64,128]{2,1,0:T(8,128)(2,1)S(1)} fusion(bf16[64,192,128]{2,0,1:T(8,128)(2,1)} %get-tuple-element.186, s32[1024]{0:T(1024)S(1)} %pad_clamp_fusion.5), kind=kCustom, calls=%fused_computation.1.clone.1 | custom fusion | bytes 1048704 | tf_op jit(solution)/shard_map/while/body/jit(_take)/gather | solution.py:50
  161.7 41.8 %all-to-all-start = ((f32[32,1,129]{2,1,0:T(1,128)}), f32[32,1,129]{2,1,0:T(1,128)S(1)}, u32[]{:S(2)}, u32[]{:S(2)}) async-start(f32[32,1,129]{2,1,0:T(1,128)} %broadcast_in_dim.54), calls=%async_computation | async-start | bytes 65536 | tf_op jit(solution)/shard_map/all_to_all | solution.py:12
  204.3 21.6 %all-to-all-done = f32[32,1,129]{2,1,0:T(1,128)S(1)} async-done(((f32[32,1,129]{2,1,0:T(1,128)}), f32[32,1,129]{2,1,0:T(1,128)S(1)}, u32[]{:S(2)}, u32[]{:S(2)}) %all-to-all-start) | async-done | bytes 16544 | tf_op jit(solution)/shard_map/all_to_all | solution.py:12
  228.0 4.6 %all-to-all-start.1 = ((f32[4,4,8]{2,1,0:T(4,128)}), f32[4,4,8]{2,1,0:T(4,128)S(1)}, u32[]{:S(2)}, u32[]{:S(2)}) async-start(f32[4,4,8]{2,1,0:T(4,128)} %broadcast_in_dim.55), calls=%async_computation.1 | async-start | bytes 16384 | tf_op jit(solution)/shard_map/all_to_all | solution.py:12
  232.6 1.1 divide_add_fusion
  233.7 4.2 %all-to-all-done.1 = f32[4,4,8]{2,1,0:T(4,128)S(1)} async-done(((f32[4,4,8]{2,1,0:T(4,128)}), f32[4,4,8]{2,1,0:T(4,128)S(1)}, u32[]{:S(2)}, u32[]{:S(2)}) %all-to-all-start.1) | async-done | bytes 544 | tf_op jit(solution)/shard_map/all_to_all | solution.py:12
  (145 shorter events, 39.3 us)
Async XLA Ops:
  1.5 9.5 %copy-start.3 = (s32[32]{0:T(128)S(1)}, s32[32]{0:T(128)}, u32[]{:S(2)}) copy-start(s32[32]{0:T(128)} %param.17) | copy-start | bytes 388
  1.5 10.2 %copy-start.1 = (f32[4096]{0:T(1024)S(1)}, f32[4096]{0:T(1024)}, u32[]{:S(2)}) copy-start(f32[4096]{0:T(1024)} %param.13) | copy-start | bytes 49156
  4.9 16.3 %collective-permute-start = (bf16[64,4096]{1,0:T(8,128)(2,1)}, bf16[64,4096]{1,0:T(8,128)(2,1)S(1)}, u32[]{:S(2)}, u32[]{:S(2)}) collective-permute-start(bf16[64,4096]{1,0:T(8,128)(2,1)} %get-tuple-element.95), channel_id=1, source_target_pairs={{0,8},{8,16},{16,24},{24,32},{32,40},{40,48},{48,56},{56,64},{64,7... | collective-permute-start | bytes 1572872 | tf_op jit(solution)/shard_map/ppermute | solution.py:37
  9.7 16.7 %collective-permute-start.1 = (bf16[64,4096]{1,0:T(8,128)(2,1)}, bf16[64,4096]{1,0:T(8,128)(2,1)}, u32[]{:S(2)}, u32[]{:S(2)}) collective-permute-start(bf16[64,4096]{1,0:T(8,128)(2,1)} %get-tuple-element.96), channel_id=1, source_target_pairs={{8,0},{16,8},{24,16},{32,24},{40,32},{48,40},{56,48},{64,56},{72,6... | collective-permute-start | bytes 1572872 | tf_op jit(solution)/shard_map/ppermute | solution.py:38
  12.3 17.1 %copy-start = (bf16[16,128,128]{2,1,0:T(8,128)(2,1)S(1)}, bf16[16,128,128]{2,1,0:T(8,128)(2,1)}, u32[]{:S(2)}) copy-start(bf16[16,128,128]{2,1,0:T(8,128)(2,1)} %param.14) | copy-start | bytes 1572868
  161.7 64.2 %all-to-all-start = ((f32[32,1,129]{2,1,0:T(1,128)}), f32[32,1,129]{2,1,0:T(1,128)S(1)}, u32[]{:S(2)}, u32[]{:S(2)}) async-start(f32[32,1,129]{2,1,0:T(1,128)} %broadcast_in_dim.54), calls=%async_computation | async-start | bytes 65536 | tf_op jit(solution)/shard_map/all_to_all | solution.py:12
  227.3 11.1 %copy-start.2 = (f32[2,4,8]{2,1,0:T(4,128)}, f32[2,4,8]{2,1,0:T(4,128)S(1)}, u32[]{:S(2)}) copy-start(f32[2,4,8]{2,1,0:T(4,128)S(1)} %div.39) | copy-start | bytes 772
  228.0 9.9 %all-to-all-start.1 = ((f32[4,4,8]{2,1,0:T(4,128)}), f32[4,4,8]{2,1,0:T(4,128)S(1)}, u32[]{:S(2)}, u32[]{:S(2)}) async-start(f32[4,4,8]{2,1,0:T(4,128)} %broadcast_in_dim.55), calls=%async_computation.1 | async-start | bytes 16384 | tf_op jit(solution)/shard_map/all_to_all | solution.py:12
where the time goes:
time: 241 us; the launch traced here: 238 us
  local copies, waits for them, and re-layouts  83.2 us (35%)
  starting transfers between devices  52.4 us (22%)
  waiting for transfers between devices  39.8 us (17%)
  other arithmetic  28.2 us (12%)
  loops' own time  17.6 us (7%)
  matrix products  16.4 us (7%)
    gather x24, local copies, waits for them, and re-layouts, one_slot(): chosen = jnp.take(source, picked[:, position], axis=1)  60.9 us
    all_to_all x2, starting transfers between devices, from_everyone(): lax.all_to_all(jnp.broadcast_to(array[None], (length, *array.shape)), axi...  46.4 us
    all_to_all x2, waiting for transfers between devices, from_everyone(): lax.all_to_all(jnp.broadcast_to(array[None], (length, *array.shape)), axi...  25.8 us
    gather x24, local copies, waits for them, and re-layouts, one_slot(): weights = jnp.take(weight_tiles, tile_ids[:, position], axis=0)  18 us
    another operation x1, loops' own time, slot_terms(): return lax.fori_loop(bounds[0], bounds[1], one_slot, start)  17.6 us
    reduce_and x24, other arithmetic, one_slot(): chosen = jnp.take(source, picked[:, position], axis=1)  17.3 us
    dot_general x24, matrix products, one_slot(): jnp.einsum('cnb,nbd->cnd', chosen, weights, preferred_element_type=jnp.fl...  16.4 us
    ppermute x1, waiting for transfers between devices, extended_2(): before = lax.ppermute(last, axis, up)  8.86 us
  transfers between devices with their start and end apart: 4, of which 4 were waited for; matrix products, arithmetic and copies ran while one was open for 1% of the time, Pallas kernels for 0%

commit v1 on v0

v1 whole, which is shorter than its diff:
```python
import functools

import jax
import jax.numpy as jnp
from jax import lax
from jax.experimental import pallas as pl
from jax.experimental.pallas import tpu as pltpu
from jax.sharding import PartitionSpec as P

MESH = pl.DeviceIdType.MESH
HALO = 32
F32, BF16, I32 = jnp.float32, jnp.bfloat16, jnp.int32
HIGHEST = lax.Precision.HIGHEST
WORDS = 384


def row_dot(a, b, precision=None):
    return lax.dot_general(
        a, b, (((1,), (1,)), ((), ())), preferred_element_type=F32, precision=precision
    )


def in_three(x):
    high = jnp.round(x * 0.25) * 4.0
    rest = x - high
    mid = jnp.round(rest * 131072.0) * (1.0 / 131072.0)
    return high, mid, rest - mid


def window(n):
    return [o for o in range(1 - n // 8, n // 8 + 1) if o != 0]


def main_kernel(
    n, mems, shape,
    surf, area, mask, tarea, tiles_in, tile_of, block_of, live_in,
    scaled_out, tot_out,
    surf_v, ext, am_v, mask_v, ta_v, w_v, idx, sm, scaled, psend, prec,
    s_msg, rxm, msg1, rx1, msg2, rx2, msg3, rx3,
    lsem, ssem, isend, irecv, msend, mrecv, s1send, s1recv, s2send, s2recv, s3send, s3recv,
    pssem, prsem, relay, relay_mem,
):
    columns, own, tgt, slots, tiles, members, reach = shape
    me = lax.axis_index("band")
    my_mem = lax.axis_index("mem")

    def band(o):
        return {"band": lax.rem(me + (o + n), n)}

    def mem(o):
        return {"mem": lax.rem(my_mem + o, mems)}

    def remote(src, dst, send, recv, where):
        return pltpu.make_async_remote_copy(
            src_ref=src, dst_ref=dst, send_sem=send, recv_sem=recv,
            device_id=where, device_id_type=MESH,
        )

    def tell(sem, where):
        pl.semaphore_signal(sem, inc=1, device_id=where, device_id_type=MESH)

    barrier = pltpu.get_barrier_semaphore()
    for where in (band(-1), band(1), mem(1), mem(mems - 1)):
        tell(barrier, where)

    loads = [
        pltpu.make_async_copy(block_of, idx.at[0, 0:slots], lsem.at[0]),
        pltpu.make_async_copy(tile_of, idx.at[0, slots : 2 * slots], lsem.at[1]),
        pltpu.make_async_copy(live_in, idx.at[0, 2 * slots : 2 * slots + 1], lsem.at[2]),
        pltpu.make_async_copy(area, am_v, lsem.at[3]),
        pltpu.make_async_copy(mask, mask_v, lsem.at[4]),
        pltpu.make_async_copy(tiles_in, w_v.at[0:tiles], lsem.at[5]),
        pltpu.make_async_copy(tarea, ta_v, lsem.at[6]),
    ]
    parts = 4
    width = own * 128 // parts
    pieces = [
        pltpu.make_async_copy(
            surf.at[:, q * width : (q + 1) * width],
            surf_v.at[:, q * width : (q + 1) * width],
            ssem.at[q],
        )
        for q in range(parts)
    ]
    for c in loads[:5] + pieces[:2] + loads[5:] + pieces[2:]:
        c.start()
    w_v[tiles] = jnp.zeros((128, 128), BF16)

    pl.semaphore_wait(barrier, 4)
    steps = [1 << i for i in range((n // 4).bit_length() - 1)]
    for where in (band(-1), band(1)):
        tell(relay.at[0], where)
    for where in (mem(1), mem(mems - 1)):
        tell(relay_mem, where)

    for c in loads[:3]:
        c.wait()
    to_low = remote(idx.at[0], idx.at[2], isend.at[0], irecv.at[0], band(-1))
    to_up = remote(idx.at[0], idx.at[1], isend.at[1], irecv.at[1], band(1))
    to_low.start()
    to_up.start()
    own_scalars = pltpu.make_async_copy(idx.at[0], sm.at[0], lsem.at[0])
    own_scalars.start()

    loads[3].wait()
    loads[4].wait()
    am_v[...] = am_v[...] * mask_v[...].astype(F32)

    def weigh(s, total):
        at = pl.ds(pl.multiple_of(s * 128, 128), 128)
        value = (am_v[pl.ds(s, 1), :] * surf_v[:, at].astype(F32)).astype(BF16)
        ext[s] = value
        return total + value.astype(F32)

    s_acc = jnp.zeros((columns, 128), F32)
    for q in range(parts):
        pieces[q].wait()
        s_acc = lax.fori_loop(q * own // parts, (q + 1) * own // parts, weigh, s_acc, unroll=4)
    ones = jnp.ones((8, 128), F32)
    s_row = row_dot(ones, s_acc, HIGHEST)[0:1]
    s_msg[...] = jnp.concatenate([s_row, jnp.zeros((1, 128 - columns), F32)], axis=1)

    pl.semaphore_wait(relay.at[0], 2)
    for where in (band(-2), band(2)):
        tell(relay.at[1], where)

    loads[5].wait()
    flat_w = w_v[0:tiles].reshape(tiles * 128, 128)
    sums = row_dot(jnp.ones((8, 128), BF16), flat_w)
    row_sums = jnp.concatenate([sums[0:1, q * 128 : (q + 1) * 128] for q in range(tiles)], axis=0)

    pl.semaphore_wait(relay_mem, 2)
    to_mem = [remote(s_msg, rxm.at[my_mem], msend.at[d], mrecv.at[my_mem], mem(d)) for d in range(1, mems)]
    for c in to_mem:
        c.start()

    to_low.wait_recv()
    to_up.wait_recv()
    far_scalars = [pltpu.make_async_copy(idx.at[i], sm.at[i], lsem.at[i]) for i in (1, 2)]
    for c in far_scalars:
        c.start()

    place = lax.broadcasted_iota(I32, (slots, tgt), 0)
    lane = lax.broadcasted_iota(I32, (slots, tgt), 1)

    def listed(i):
        block = idx[i, 0:slots, :]
        tile = idx[i, slots : 2 * slots, :]
        alive = place < idx[i, 2 * slots : 2 * slots + 1, :]
        return block, jnp.where(alive, tile, -1)

    b0, w0 = listed(0)
    b1, w1 = listed(1)
    b2, w2 = listed(2)
    has_low = me > 0
    has_up = me < n - 1
    from_low = (lane >= tgt - reach) & has_low
    from_up = (lane < reach) & has_up
    blocks_ = (b0 - HALO, jnp.where(from_low, b1 - (HALO + own), b2 - HALO + own))
    tiles_ = (w0, jnp.where(from_low, w1, jnp.where(from_up, w2, -1)))

    def flat(pair):
        return jnp.concatenate([x[k : k + 1] for x in pair for k in range(slots)], axis=1)

    total_slots = 2 * slots * tgt
    block_row, tile_row = flat(blocks_), flat(tiles_)
    at_block = (lax.broadcasted_iota(I32, (own, total_slots), 0) == block_row).astype(F32).astype(BF16)
    at_tile = (lax.broadcasted_iota(I32, (tiles, total_slots), 0) == tile_row).astype(F32).astype(BF16)
    count = row_dot(at_block, at_tile)
    reach_sum = lax.dot_general(
        count, row_sums, (((1,), (0,)), ((), ())), preferred_element_type=F32, precision=HIGHEST
    )
    mask_v_f = am_v
    mask_v_f[...] = reach_sum

    def weigh_target(s, total):
        return total + ext[s].astype(F32) * mask_v_f[pl.ds(s, 1), :]

    t_acc = lax.fori_loop(0, own, weigh_target, jnp.zeros((columns, 128), F32), unroll=4)
    t_row = row_dot(ones, t_acc, HIGHEST)[0:1]

    pl.semaphore_wait(relay.at[1], 2)
    for where in (band(-4), band(4)):
        tell(relay.at[2], where)

    loads[6].wait()
    rxm[my_mem] = s_msg[...]
    for d in range(1, mems):
        other = lax.rem(my_mem + d, mems)
        remote(s_msg, rxm.at[other], msend.at[d], mrecv.at[other], mem(d)).wait_recv()
    e_row = rxm[0]
    for m in range(1, mems):
        e_row = e_row + rxm[m]
    per = columns // members
    e_sum = e_row[:, 0:per]
    for m in range(1, members):
        e_sum = e_sum + e_row[:, m * per : (m + 1) * per]
    a_sum = jnp.sum(jnp.sum(ta_v[...], axis=0, keepdims=True), axis=1, keepdims=True)
    a_high = jnp.round(a_sum * 64.0) * (1.0 / 64.0)
    s_parts, e_parts = in_three(s_row), in_three(e_sum)
    used = 4 * columns + 3 * per + 2
    msg1[...] = jnp.concatenate(
        [s_parts[0], t_row, s_parts[1], s_parts[2], *e_parts, a_high, a_sum - a_high,
         jnp.zeros((1, WORDS - used), F32)],
        axis=1,
    )

    offsets = window(n)
    first = [remote(msg1, rx1.at[i], s1send.at[i], s1recv.at[i], band(-o)) for i, o in enumerate(offsets)]
    for c in first:
        c.start()

    def slot_sum(which, t, shift, alive):
        live = sm[which, 2 * slots, t] * alive
        total = None
        for p in range(slots // 2):
            left, right = [], []
            for k in (2 * p, 2 * p + 1):
                block = sm[which, k, t] + shift
                good = (k < live) & (block >= 0) & (block < own)
                left.append(ext[jnp.clip(block, 0, own - 1)])
                right.append(w_v[jnp.where(good, sm[which, slots + k, t], tiles)])
            term = jnp.dot(
                jnp.concatenate(left, axis=1), jnp.concatenate(right, axis=0), preferred_element_type=F32
            )
            total = term if total is None else total + term
        return total

    own_scalars.wait()
    for c in far_scalars:
        c.wait()

    def part_copy(side, i):
        return remote(
            psend.at[side, i], prec.at[1 - side, i], pssem.at[side, i], prsem.at[1 - side, i],
            band(2 * side - 1),
        )

    def for_neighbours(i, carry):
        psend[0, i] = slot_sum(1, tgt - reach + i, -(HALO + own), has_low.astype(I32))
        psend[1, i] = slot_sum(2, i, own - HALO, has_up.astype(I32))

        @pl.when(i > 0)
        def _():
            part_copy(0, i - 1).start()
            part_copy(1, i - 1).start()

        return carry

    lax.fori_loop(0, reach, for_neighbours, 0)
    for side in (0, 1):
        part_copy(side, reach - 1).start()

    for c in first:
        c.wait_recv()
    running = msg1[...]
    for i in range(len(offsets)):
        running = running + rx1[i]
    msg2[...] = running
    second = [remote(msg2, rx2.at[i], s2send.at[i], s2recv.at[i], band(o)) for i, o in enumerate((-(n // 8), n // 8))]
    for c in second:
        c.start()

    def keep(t, value):
        at = pl.ds(pl.multiple_of(t * 128, 128), 128)
        scaled[:, at] = value / ta_v[pl.ds(t, 1), :]

    def inner(t, carry):
        keep(t, slot_sum(0, t, -HALO, 1))
        return carry

    def put(start, stop, sem):
        c = pltpu.make_async_copy(
            scaled.at[:, start * 128 : stop * 128], scaled_out.at[:, start * 128 : stop * 128], sem
        )
        c.start()
        return c

    lax.fori_loop(reach, tgt - reach, inner, 0)
    puts = [put(reach, tgt - reach, ssem.at[0])]

    for c in second:
        c.wait_recv()
    msg3[...] = rx2[0] + rx2[1]
    pl.semaphore_wait(relay.at[2], 2)
    third = [remote(msg3, rx3.at[i], s3send.at[i], s3recv.at[i], band(o)) for i, o in enumerate((-(n // 4), n // 4))]
    for c in third:
        c.start()

    def edge(i, carry):
        low = slot_sum(0, i, -HALO, 1)
        up = slot_sum(0, tgt - reach + i, -HALO, 1)
        part_copy(1, i).wait_recv()
        part_copy(0, i).wait_recv()
        keep(i, low + prec[0, i])
        keep(tgt - reach + i, up + prec[1, i])
        return carry

    lax.fori_loop(0, reach, edge, 0)
    puts.append(put(0, reach, ssem.at[1]))
    puts.append(put(tgt - reach, tgt, ssem.at[2]))

    for c in third:
        c.wait_recv()
    tot_out[...] = rx3[0] + rx3[1]
    for c in [to_low, to_up, *to_mem, *first, *second, *third]:
        c.wait_send()

    def sent(i, carry):
        part_copy(0, i).wait_send()
        part_copy(1, i).wait_send()
        return carry

    lax.fori_loop(0, reach, sent, 0)
    for c in puts:
        c.wait()


def last_kernel(shape, mems, tot, scaled, out, conserved, ensemble, fix):
    columns, members, fields, snaps = shape
    per = columns // members

    @pl.when(pl.program_id(0) == 0)
    def _():
        def at(start, size):
            return tot[:, start : start + size]

        base = 4 * columns
        s = (at(0, columns) + at(2 * columns, columns)) + at(3 * columns, columns)
        e = (at(base, per) + at(base + per, per)) + at(base + 2 * per, per)
        total_area = at(base + 3 * per, 1) + at(base + 3 * per + 1, 1)
        step = (s - at(columns, columns)) / total_area
        diagonal = lax.broadcasted_iota(I32, (columns, columns), 0) == lax.broadcasted_iota(
            I32, (columns, columns), 1
        )
        column = jnp.sum(jnp.where(diagonal, step, 0.0), axis=1, keepdims=True)
        fix[...] = jnp.broadcast_to(column, (columns, 128))
        mean = s / total_area
        for i in range(members * fields):
            conserved[i // fields, i % fields : i % fields + 1, :] = mean[:, i * snaps : (i + 1) * snaps]
        group = e / total_area / float(members * mems)
        for f in range(fields):
            ensemble[f : f + 1, :] = group[:, f * snaps : (f + 1) * snaps]

    for b in range(out.shape[1] // 128):
        out[:, b * 128 : (b + 1) * 128] = scaled[:, b * 128 : (b + 1) * 128] + fix[...]


def on_device(n, mems, surf, mask, area, tarea, tiles_in, tile_of, block_of, live):
    members, fields, snaps, cells = surf.shape
    columns = members * fields * snaps
    own = cells // 128
    tgt, slots = tile_of.shape
    tiles = tiles_in.shape[0]
    reach = HALO * tgt // own
    any_space = pl.BlockSpec(memory_space=pl.ANY)
    dma, plain = pltpu.SemaphoreType.DMA, pltpu.SemaphoreType.REGULAR
    rows = -(-(2 * slots + 1) // 8) * 8
    count = len(window(n))
    scaled, tot = pl.pallas_call(
        functools.partial(main_kernel, n, mems, (columns, own, tgt, slots, tiles, members, reach)),
        out_shape=(
            jax.ShapeDtypeStruct((columns, tgt * 128), F32),
            jax.ShapeDtypeStruct((1, WORDS), F32),
        ),
        in_specs=[any_space] * 8,
        out_specs=(any_space, pl.BlockSpec(memory_space=pltpu.VMEM)),
        scratch_shapes=[
            pltpu.VMEM((columns, cells), BF16),
            pltpu.VMEM((own, columns, 128), BF16),
            pltpu.VMEM((own, 128), F32),
            pltpu.VMEM((own, 128), I32),
            pltpu.VMEM((tgt, 128), F32),
            pltpu.VMEM((tiles + 1, 128, 128), BF16),
            pltpu.VMEM((3, rows, tgt), I32),
            pltpu.SMEM((3, rows, tgt), I32),
            pltpu.VMEM((columns, tgt * 128), F32),
            pltpu.VMEM((2, reach, columns, 128), F32),
            pltpu.VMEM((2, reach, columns, 128), F32),
            pltpu.VMEM((1, 128), F32),
            pltpu.VMEM((mems, 1, 128), F32),
            pltpu.VMEM((1, WORDS), F32),
            pltpu.VMEM((count, 1, WORDS), F32),
            pltpu.VMEM((1, WORDS), F32),
            pltpu.VMEM((2, 1, WORDS), F32),
            pltpu.VMEM((1, WORDS), F32),
            pltpu.VMEM((2, 1, WORDS), F32),
            dma((7,)), dma((4,)), dma((2,)), dma((2,)), dma((mems,)), dma((mems,)),
            dma((count,)), dma((count,)), dma((2,)), dma((2,)), dma((2,)), dma((2,)),
            dma((2, reach)), dma((2, reach)), plain((3,)), plain,
        ],
        compiler_params=pltpu.CompilerParams(collective_id=0, has_side_effects=True),
        name="regrid",
    )(
        surf.reshape(columns, cells),
        area.reshape(own, 128),
        mask.reshape(own, 128),
        tarea.reshape(tgt, 128),
        tiles_in,
        tile_of.T,
        block_of.T,
        live.reshape(1, tgt),
    )
    steps = 4
    wide = tgt * 128 // steps
    whole = lambda *dims: pl.BlockSpec(dims, lambda i: (0,) * len(dims))
    out, conserved, ensemble = pl.pallas_call(
        functools.partial(last_kernel, (columns, members, fields, snaps), mems),
        grid=(steps,),
        out_shape=(
            jax.ShapeDtypeStruct((columns, tgt * 128), F32),
            jax.ShapeDtypeStruct((members, fields, snaps), F32),
            jax.ShapeDtypeStruct((fields, snaps), F32),
        ),
        in_specs=[whole(1, WORDS), pl.BlockSpec((columns, wide), lambda i: (0, i))],
        out_specs=(
            pl.BlockSpec((columns, wide), lambda i: (0, i)),
            whole(members, fields, snaps),
            whole(fields, snaps),
        ),
        scratch_shapes=[pltpu.VMEM((columns, 128), F32)],
        name="finish",
    )(tot, scaled)
    return out.reshape(members, fields, snaps, tgt * 128), conserved, ensemble


def solution(mesh):
    placed = (
        P(("grp", "mem"), "fld", None, "band"),
        P("band"),
        P("band"),
        P("band"),
        P(),
        P("band", None),
        P("band", None),
        P("band"),
    )
    return jax.shard_map(
        functools.partial(on_device, mesh.shape["band"], mesh.shape["mem"]),
        mesh=mesh,
        in_specs=placed,
        out_specs=(
            P(("grp", "mem"), "fld", None, "band"),
            P(("grp", "mem"), "fld", None),
            P(("grp", "fld"), None),
        ),
        check_vma=False,
    )
```

time: 241 us -> 72.8 us (0.30)
  local copies, waits for them, and re-layouts: 83.2 us -> 0 us
  Pallas kernels: 0 us -> 71.9 us
  starting transfers between devices: 52.4 us -> 0 us
  waiting for transfers between devices: 39.8 us -> 0 us
  other arithmetic: 28.2 us -> 0 us
  loops' own time: 17.6 us -> 0 us
  matrix products: 16.4 us -> 0 us
    gather x48 -> x0, local copies, waits for them, and re-layouts: 78.9 us -> none  [the longest x24 60.9 us: one_slot(): chosen = jnp.take(source, picked[:, position], axis=1)]
    pallas_call x0 -> x2, Pallas kernels: none -> 71.9 us  [the longest x1 68.3 us: on_device(): pl.pallas_call(functools.partial(main_kernel, n, mems, (columns, own, tgt...]
    all_to_all x2 -> x0, starting transfers between devices: 46.4 us -> none  [from_everyone(): lax.all_to_all(jnp.broadcast_to(array[None], (length, *array.shape)), axi...]
    all_to_all x2 -> x0, waiting for transfers between devices: 25.8 us -> none  [from_everyone(): lax.all_to_all(jnp.broadcast_to(array[None], (length, *array.shape)), axi...]
    another operation x1 -> x0, loops' own time: 17.6 us -> none  [slot_terms(): return lax.fori_loop(bounds[0], bounds[1], one_slot, start)]
    reduce_and x24 -> x0, other arithmetic: 17.3 us -> none  [one_slot(): chosen = jnp.take(source, picked[:, position], axis=1)]
    dot_general x24 -> x0, matrix products: 16.4 us -> none  [one_slot(): jnp.einsum('cnb,nbd->cnd', chosen, weights, preferred_element_type=jnp.fl...]
    ppermute x2 -> x0, waiting for transfers between devices: 14.1 us -> none  [the longest x1 8.86 us: extended_2(): before = lax.ppermute(last, axis, up)]
  transfers between devices with their start and end apart: 4 -> 0, of which waited for: 4 -> 0; matrix products, arithmetic and copies ran while one was open for 1% -> 0% of each run, Pallas kernels for 0% -> 0%
where the time goes in v1:
time: 72.8 us; the launch traced here: 72.6 us
  Pallas kernels  71.9 us (99%)
    pallas_call x1, Pallas kernels, on_device(): pl.pallas_call(functools.partial(main_kernel, n, mems, (columns, own, tgt...  68.3 us
    pallas_call x1, Pallas kernels, on_device(): pl.pallas_call(functools.partial(last_kernel, (columns, members, fields,...  3.64 us

profile of v1, /device:TPU:40, one launch (start us, length us, event | category | flops | bytes accessed | tf_op | source)
XLA Modules:
  0.0 72.6 jit_solution(15661654453874787602)
XLA Ops:
  0.6 68.3 %regrid.1 = (f32[64,4096]{1,0:T(8,128)}, f32[1,384]{1,0:T(1,128)}) custom-call(bf16[64,16384]{1,0:T(8,128)(2,1)} %bitcast.8, f32[128,128]{1,0:T(8,128)} %bitcast.9, s32[128,128]{1,0:T(8,128)} %bitcast.10, f32[32,128]{1,0:T(8,128)} %bitcast.11, bf16[16,128,128]{2,1,0:T(8,128)(2,1)} %tiles_in.1, s32[24,32]{1,0:T(8,128)} %bitcast.12, s32[24,32]{1,0:T(8,128)} %bitcast.13, ...), custom_call_target="tpu_custom_call" | custom-call | tf_op jit(solution)/shard_map/regrid/pallas_call | solution.py:360
  68.9 3.6 %finish.1 = (f32[64,4096]{1,0:T(8,128)}, f32[2,4,8]{2,1,0:T(4,128)}, f32[4,8]{1,0:T(4,128)}) custom-call(f32[1,384]{1,0:T(1,128)} %get-tuple-element.8.tot, f32[64,4096]{1,0:T(8,128)} %get-tuple-element.9.scaled), custom_call_target="tpu_custom_call" | custom-call | tf_op jit(solution)/shard_map/finish/pallas_call | solution.py:407

commit v2 on v1

v2 whole, which is shorter than its diff:
```python
import functools

import jax
import jax.numpy as jnp
from jax import lax
from jax.experimental import pallas as pl
from jax.experimental.pallas import tpu as pltpu
from jax.sharding import PartitionSpec as P

MESH = pl.DeviceIdType.MESH
HALO = 32
F32, BF16, I32 = jnp.float32, jnp.bfloat16, jnp.int32
HIGHEST = lax.Precision.HIGHEST
WORDS = 384


def row_dot(a, b, precision=None):
    return lax.dot_general(
        a, b, (((1,), (1,)), ((), ())), preferred_element_type=F32, precision=precision
    )


def in_three(x):
    high = jnp.round(x * 0.25) * 4.0
    rest = x - high
    mid = jnp.round(rest * 131072.0) * (1.0 / 131072.0)
    return high, mid, rest - mid


def main_kernel(
    n, mems, shape,
    surf, area, mask, tarea, tiles_in, tile_of, block_of, live_in,
    scaled, tot_out,
    surf_v, ext, am_v, mask_v, ta_v, w_v, idx, sm, s_acc, reach_sum, psend, prec,
    s_msg, rxm, msg, rx, rxw, run, rxp,
    lsem, ssem, isend, irecv, msend, mrecv, dsend, drecv, wsend, wrecv, csend, crecv,
    pssem, prsem, upper_in, lower_in, mem_in,
):
    columns, own, tgt, slots, tiles, members, reach = shape
    me = lax.axis_index("band")
    my_mem = lax.axis_index("mem")
    has_low = me > 0
    has_up = me < n - 1
    half = n // 2

    def band(o):
        return {"band": me + o}

    def mem(o):
        return {"mem": lax.rem(my_mem + o, mems)}

    def remote(src, dst, send, recv, where):
        return pltpu.make_async_remote_copy(
            src_ref=src, dst_ref=dst, send_sem=send, recv_sem=recv,
            device_id=where, device_id_type=MESH,
        )

    def tell(sem, where):
        pl.semaphore_signal(sem, inc=1, device_id=where, device_id_type=MESH)

    barrier = pltpu.get_barrier_semaphore()

    @pl.when(has_low)
    def _():
        tell(barrier, band(-1))

    @pl.when(has_up)
    def _():
        tell(barrier, band(1))

    for where in (mem(1), mem(mems - 1)):
        tell(barrier, where)

    loads = [
        pltpu.make_async_copy(block_of, idx.at[0, 0:slots], lsem.at[0]),
        pltpu.make_async_copy(tile_of, idx.at[0, slots : 2 * slots], lsem.at[1]),
        pltpu.make_async_copy(live_in, idx.at[0, 2 * slots : 2 * slots + 1], lsem.at[2]),
        pltpu.make_async_copy(area, am_v, lsem.at[3]),
        pltpu.make_async_copy(mask, mask_v, lsem.at[4]),
        pltpu.make_async_copy(tiles_in, w_v.at[0:tiles], lsem.at[5]),
        pltpu.make_async_copy(tarea, ta_v, lsem.at[6]),
    ]
    parts = 4
    width = own * 128 // parts
    pieces = [
        pltpu.make_async_copy(
            surf.at[:, q * width : (q + 1) * width],
            surf_v.at[:, q * width : (q + 1) * width],
            ssem.at[q],
        )
        for q in range(parts)
    ]
    for c in loads[:5] + pieces[:2] + loads[5:] + pieces[2:]:
        c.start()
    w_v[tiles] = jnp.zeros((128, 128), BF16)
    for c in loads[:3]:
        c.wait()
    scalars = [pltpu.make_async_copy(idx.at[i], sm.at[i], lsem.at[i]) for i in range(3)]
    scalars[0].start()

    def weigh(s, total):
        at = pl.ds(pl.multiple_of(s * 128, 128), 128)
        value = (am_v[pl.ds(s, 1), :] * surf_v[:, at].astype(F32)).astype(BF16)
        ext[s] = value
        return total + value.astype(F32)

    def local_part():
        loads[3].wait()
        loads[4].wait()
        am_v[...] = am_v[...] * mask_v[...].astype(F32)
        total = jnp.zeros((columns, 128), F32)
        for q in range(parts):
            pieces[q].wait()
            total = lax.fori_loop(q * own // parts, (q + 1) * own // parts, weigh, total, unroll=4)
        s_acc[...] = total
        loads[5].wait()
        loads[6].wait()
        scalars[0].wait()

    def slot_sum(which, t, shift, alive):
        live = sm[which, 2 * slots, t] * alive
        total = None
        for p in range(slots // 2):
            left, right = [], []
            for k in (2 * p, 2 * p + 1):
                block = sm[which, k, t] + shift
                good = (k < live) & (block >= 0) & (block < own)
                left.append(ext[jnp.clip(block, 0, own - 1)])
                right.append(w_v[jnp.where(good, sm[which, slots + k, t], tiles)])
            term = jnp.dot(
                jnp.concatenate(left, axis=1), jnp.concatenate(right, axis=0), preferred_element_type=F32
            )
            total = term if total is None else total + term
        return total

    def columns_of(t):
        return pl.ds(pl.multiple_of(t * 128, 128), 128)

    def own_targets():
        def body(t, carry):
            scaled[:, columns_of(t)] = slot_sum(0, t, -HALO, 1)
            return carry

        lax.fori_loop(0, tgt, body, 0)

    @pl.when(me == 0)
    def _():
        local_part()
        own_targets()

    near = has_low.astype(I32) + has_up.astype(I32)
    pl.semaphore_wait(barrier, near + 2)
    to_low = remote(idx.at[0], idx.at[2], isend.at[0], irecv.at[0], band(-1))
    to_up = remote(idx.at[0], idx.at[1], isend.at[1], irecv.at[1], band(1))

    @pl.when(has_low)
    def _():
        to_low.start()
        tell(upper_in, band(-1))

    @pl.when(has_up)
    def _():
        to_up.start()

    for where in (mem(1), mem(mems - 1)):
        tell(mem_in, where)

    @pl.when(me > 1)
    def _():
        pl.semaphore_wait(lower_in, 1)

    @pl.when((me > 0) & has_up)
    def _():
        tell(lower_in, band(1))

    @pl.when(has_low)
    def _():
        local_part()

    @pl.when(has_low & (me < half))
    def _():
        own_targets()

    ones = jnp.ones((8, 128), F32)
    s_row = row_dot(ones, s_acc[...], HIGHEST)[0:1]
    s_msg[...] = jnp.concatenate([s_row, jnp.zeros((1, 128 - columns), F32)], axis=1)

    flat_w = w_v[0:tiles].reshape(tiles * 128, 128)
    sums = row_dot(jnp.ones((8, 128), BF16), flat_w)
    row_sums = jnp.concatenate([sums[0:1, q * 128 : (q + 1) * 128] for q in range(tiles)], axis=0)

    pl.semaphore_wait(mem_in, 2)
    to_mem = [remote(s_msg, rxm.at[my_mem], msend.at[d], mrecv.at[my_mem], mem(d)) for d in range(1, mems)]
    for c in to_mem:
        c.start()

    place = lax.broadcasted_iota(I32, (slots, tgt), 0)
    lane = lax.broadcasted_iota(I32, (slots, tgt), 1)

    def listed(i):
        block = idx[i, 0:slots, :]
        tile = idx[i, slots : 2 * slots, :]
        alive = place < idx[i, 2 * slots : 2 * slots + 1, :]
        return block, jnp.where(alive, tile, -1)

    def cell_sums(block, tile):
        count = slots * tgt
        block_row = jnp.concatenate([block[k : k + 1] for k in range(slots)], axis=1)
        tile_row = jnp.concatenate([tile[k : k + 1] for k in range(slots)], axis=1)
        at_block = (lax.broadcasted_iota(I32, (own, count), 0) == block_row).astype(F32).astype(BF16)
        at_tile = (lax.broadcasted_iota(I32, (tiles, count), 0) == tile_row).astype(F32).astype(BF16)
        return lax.dot_general(
            row_dot(at_block, at_tile), row_sums, (((1,), (0,)), ((), ())),
            preferred_element_type=F32, precision=HIGHEST,
        )

    def weigh_target(s, total):
        return total + ext[s].astype(F32) * reach_sum[pl.ds(s, 1), :]

    b0, w0 = listed(0)
    reach_sum[...] = cell_sums(b0 - HALO, w0)
    t_acc = lax.fori_loop(0, own, weigh_target, jnp.zeros((columns, 128), F32), unroll=4)

    @pl.when(has_low)
    def _():
        to_up.wait_recv()
        scalars[1].start()

    @pl.when(has_up)
    def _():
        to_low.wait_recv()
        scalars[2].start()

    b1, w1 = listed(1)
    b2, w2 = listed(2)
    from_low = (lane >= tgt - reach) & has_low
    from_up = (lane < reach) & has_up
    reach_sum[...] = cell_sums(
        jnp.where(from_low, b1 - (HALO + own), b2 - HALO + own),
        jnp.where(from_low, w1, jnp.where(from_up, w2, -1)),
    )
    t_acc = lax.fori_loop(0, HALO, weigh_target, t_acc, unroll=4)
    t_acc = lax.fori_loop(own - HALO, own, weigh_target, t_acc, unroll=4)
    t_row = row_dot(ones, t_acc, HIGHEST)[0:1]

    rxm[my_mem] = s_msg[...]
    for d in range(1, mems):
        other = lax.rem(my_mem + d, mems)
        remote(s_msg, rxm.at[other], msend.at[d], mrecv.at[other], mem(d)).wait_recv()
    e_row = rxm[0]
    for m in range(1, mems):
        e_row = e_row + rxm[m]
    per = columns // members
    e_sum = e_row[:, 0:per]
    for m in range(1, members):
        e_sum = e_sum + e_row[:, m * per : (m + 1) * per]
    a_sum = jnp.sum(jnp.sum(ta_v[...], axis=0, keepdims=True), axis=1, keepdims=True)
    a_high = jnp.round(a_sum * 64.0) * (1.0 / 64.0)
    s_parts, e_parts = in_three(s_row), in_three(e_sum)
    used = 4 * columns + 3 * per + 2
    msg[...] = jnp.concatenate(
        [s_parts[0], t_row, s_parts[1], s_parts[2], *e_parts, a_high, a_sum - a_high,
         jnp.zeros((1, WORDS - used), F32)],
        axis=1,
    )

    def direct(q):
        return remote(msg, rx.at[me], dsend.at[q], drecv.at[me], {"band": q})

    def send_down(q, carry):
        direct(q).start()
        return carry

    lax.fori_loop(0, me, send_down, 0)

    stride = n // 8

    @pl.when(has_up)
    def _():
        for _ in range(stride - 2):
            pl.semaphore_wait(upper_in, 1)

            @pl.when(has_low)
            def _():
                tell(upper_in, band(-1))

        pl.semaphore_wait(upper_in, 1)

    @pl.when(me == n - 1)
    def _():
        for _ in range(stride - 2):
            tell(upper_in, band(-1))

    ups = [remote(msg, rxw.at[o - 1], wsend.at[o - 1], wrecv.at[o - 1], band(o)) for o in range(1, stride)]
    for o, c in enumerate(ups, 1):
        pl.when(me + o < n)(c.start)

    @pl.when(has_low)
    def _():
        scalars[1].wait()

    @pl.when(has_up)
    def _():
        scalars[2].wait()

    def part_copy(side, i):
        return remote(
            psend.at[side, i], prec.at[1 - side, i], pssem.at[side, i], prsem.at[1 - side, i],
            band(2 * side - 1),
        )

    def for_side(side):
        def body(i, carry):
            if side == 0:
                psend[0, i] = slot_sum(1, tgt - reach + i, -(HALO + own), 1)
            else:
                psend[1, i] = slot_sum(2, i, own - HALO, 1)

            @pl.when(i > 0)
            def _():
                part_copy(side, i - 1).start()

            return carry

        lax.fori_loop(0, reach, body, 0)
        part_copy(side, reach - 1).start()

    pl.when(has_low)(functools.partial(for_side, 0))
    pl.when(has_up)(functools.partial(for_side, 1))

    @pl.when(me >= half)
    def _():
        own_targets()

    def add_part(side, start):
        def body(i, carry):
            part_copy(1 - side, i).wait_recv()
            at = columns_of(start + i)
            scaled[:, at] = scaled[:, at] + prec[side, i]
            return carry

        lax.fori_loop(0, reach, body, 0)

    def divide(t, carry):
        at = columns_of(t)
        scaled[:, at] = scaled[:, at] / ta_v[pl.ds(t, 1), :]
        return carry

    pl.when(has_low)(functools.partial(add_part, 0, 0))
    pl.when(has_up)(functools.partial(add_part, 1, tgt - reach))
    lax.fori_loop(0, tgt, divide, 0)

    run[...] = msg[...]
    for o, c in enumerate(ups, 1):
        @pl.when(me >= o)
        def _():
            c.wait_recv()
            run[...] = run[...] + rxw[o - 1]

    chain = remote(run, rxp, csend, crecv, band(stride))

    @pl.when(me >= stride)
    def _():
        chain.wait_recv()
        run[...] = run[...] + rxp[...]

    pl.when(me + stride < n)(chain.start)

    def add_upper(q, total):
        remote(msg, rx.at[q], dsend.at[0], drecv.at[q], {"band": q}).wait_recv()
        return total + rx[q]

    tot_out[...] = lax.fori_loop(me + 1, n, add_upper, run[...])

    def sent(q, carry):
        direct(q).wait_send()
        return carry

    lax.fori_loop(0, me, sent, 0)
    pl.when(me + stride < n)(chain.wait_send)
    for o, c in enumerate(ups, 1):
        pl.when(me + o < n)(c.wait_send)
    for c in to_mem:
        c.wait_send()

    def parts_sent(side):
        def body(i, carry):
            part_copy(side, i).wait_send()
            return carry

        lax.fori_loop(0, reach, body, 0)

    @pl.when(has_low)
    def _():
        to_low.wait_send()
        parts_sent(0)

    @pl.when(has_up)
    def _():
        to_up.wait_send()
        parts_sent(1)


def last_kernel(shape, mems, tot, scaled, out, conserved, ensemble, done, sems):
    columns, members, fields, snaps = shape
    per = columns // members

    def at(start, size):
        return tot[:, start : start + size]

    base = 4 * columns
    s = (at(0, columns) + at(2 * columns, columns)) + at(3 * columns, columns)
    e = (at(base, per) + at(base + per, per)) + at(base + 2 * per, per)
    total_area = at(base + 3 * per, 1) + at(base + 3 * per + 1, 1)
    step = (s - at(columns, columns)) / total_area
    diagonal = lax.broadcasted_iota(I32, (columns, columns), 0) == lax.broadcasted_iota(
        I32, (columns, columns), 1
    )
    fix = jnp.broadcast_to(jnp.sum(jnp.where(diagonal, step, 0.0), axis=1, keepdims=True), (columns, 128))
    pieces = 4
    width = out.shape[1] // pieces
    copies = []
    for q in range(pieces):
        for b in range(q * width // 128, (q + 1) * width // 128):
            done[:, b * 128 : (b + 1) * 128] = scaled[:, b * 128 : (b + 1) * 128] + fix
        where = (slice(None), slice(q * width, (q + 1) * width))
        copies.append(pltpu.make_async_copy(done.at[where], out.at[where], sems.at[q]))
        copies[-1].start()
    mean = s / total_area
    for i in range(members * fields):
        conserved[i // fields, i % fields : i % fields + 1, :] = mean[:, i * snaps : (i + 1) * snaps]
    group = e / total_area / float(members * mems)
    for f in range(fields):
        ensemble[f : f + 1, :] = group[:, f * snaps : (f + 1) * snaps]
    for c in copies:
        c.wait()


def on_device(n, mems, surf, mask, area, tarea, tiles_in, tile_of, block_of, live):
    members, fields, snaps, cells = surf.shape
    columns = members * fields * snaps
    own = cells // 128
    tgt, slots = tile_of.shape
    tiles = tiles_in.shape[0]
    reach = HALO * tgt // own
    any_space = pl.BlockSpec(memory_space=pl.ANY)
    dma, plain = pltpu.SemaphoreType.DMA, pltpu.SemaphoreType.REGULAR
    rows = -(-(2 * slots + 1) // 8) * 8
    stride = n // 8
    scaled, tot = pl.pallas_call(
        functools.partial(main_kernel, n, mems, (columns, own, tgt, slots, tiles, members, reach)),
        out_shape=(pltpu.VMEM((columns, tgt * 128), F32), pltpu.VMEM((1, WORDS), F32)),
        in_specs=[any_space] * 8,
        out_specs=(pl.BlockSpec(memory_space=pltpu.VMEM),) * 2,
        scratch_shapes=[
            pltpu.VMEM((columns, cells), BF16),
            pltpu.VMEM((own, columns, 128), BF16),
            pltpu.VMEM((own, 128), F32),
            pltpu.VMEM((own, 128), I32),
            pltpu.VMEM((tgt, 128), F32),
            pltpu.VMEM((tiles + 1, 128, 128), BF16),
            pltpu.VMEM((3, rows, tgt), I32),
            pltpu.SMEM((3, rows, tgt), I32),
            pltpu.VMEM((columns, 128), F32),
            pltpu.VMEM((own, 128), F32),
            pltpu.VMEM((2, reach, columns, 128), F32),
            pltpu.VMEM((2, reach, columns, 128), F32),
            pltpu.VMEM((1, 128), F32),
            pltpu.VMEM((mems, 1, 128), F32),
            pltpu.VMEM((1, WORDS), F32),
            pltpu.VMEM((n, 1, WORDS), F32),
            pltpu.VMEM((stride - 1, 1, WORDS), F32),
            pltpu.VMEM((1, WORDS), F32),
            pltpu.VMEM((1, WORDS), F32),
            dma((7,)), dma((4,)), dma((2,)), dma((2,)), dma((mems,)), dma((mems,)),
            dma((n,)), dma((n,)), dma((stride - 1,)), dma((stride - 1,)), dma, dma,
            dma((2, reach)), dma((2, reach)), plain, plain, plain,
        ],
        compiler_params=pltpu.CompilerParams(collective_id=0, has_side_effects=True),
        name="regrid",
    )(
        surf.reshape(columns, cells),
        area.reshape(own, 128),
        mask.reshape(own, 128),
        tarea.reshape(tgt, 128),
        tiles_in,
        tile_of.T,
        block_of.T,
        live.reshape(1, tgt),
    )
    inside = pl.BlockSpec(memory_space=pltpu.VMEM)
    out, conserved, ensemble = pl.pallas_call(
        functools.partial(last_kernel, (columns, members, fields, snaps), mems),
        out_shape=(
            jax.ShapeDtypeStruct((columns, tgt * 128), F32),
            jax.ShapeDtypeStruct((members, fields, snaps), F32),
            jax.ShapeDtypeStruct((fields, snaps), F32),
        ),
        in_specs=[inside, inside],
        out_specs=(any_space, inside, inside),
        scratch_shapes=[pltpu.VMEM((columns, tgt * 128), F32), dma((4,))],
        name="finish",
    )(tot, scaled)
    return out.reshape(members, fields, snaps, tgt * 128), conserved, ensemble


def solution(mesh):
    placed = (
        P(("grp", "mem"), "fld", None, "band"),
        P("band"),
        P("band"),
        P("band"),
        P(),
        P("band", None),
        P("band", None),
        P("band"),
    )
    return jax.shard_map(
        functools.partial(on_device, mesh.shape["band"], mesh.shape["mem"]),
        mesh=mesh,
        in_specs=placed,
        out_specs=(
            P(("grp", "mem"), "fld", None, "band"),
            P(("grp", "mem"), "fld", None),
            P(("grp", "fld"), None),
        ),
        check_vma=False,
    )
```

time: 72.8 us -> 89.5 us (1.23)
  the two profiles are of different devices: /device:TPU:40 before, /device:TPU:34 now
where the time goes in v2:
time: 89.5 us; the launch traced here: 89.3 us
  Pallas kernels  87.1 us (97%)
  local copies, waits for them, and re-layouts  1.55 us (2%)
    pallas_call x1, Pallas kernels, on_device(): pl.pallas_call(functools.partial(main_kernel, n, mems, (columns, own, tgt...  84 us
    pallas_call x1, Pallas kernels, on_device(): pl.pallas_call(functools.partial(last_kernel, (columns, members, fields,...  3.11 us

profile of v2, /device:TPU:34, one launch (start us, length us, event | category | flops | bytes accessed | tf_op | source)
XLA Modules:
  0.0 89.3 jit_solution(9350516363671454175)
XLA Ops:
  0.6 84.0 %regrid.1 = (f32[64,4096]{1,0:T(8,128)S(1)}, f32[1,384]{1,0:T(1,128)S(1)}) custom-call(bf16[64,16384]{1,0:T(8,128)(2,1)} %bitcast.8, f32[128,128]{1,0:T(8,128)} %bitcast.9, s32[128,128]{1,0:T(8,128)} %bitcast.10, f32[32,128]{1,0:T(8,128)} %bitcast.11, bf16[16,128,128]{2,1,0:T(8,128)(2,1)} %tiles_in.1, s32[24,32]{1,0:T(8,128)} %bitcast.12, ...), custom_call_target="tpu_custom_call" | custom-call | tf_op jit(solution)/shard_map/regrid/pallas_call | solution.py:450
  84.7 0.0 copy-start
  84.7 1.0 %copy-done = f32[64,4096]{1,0:T(8,128)} copy-done((f32[64,4096]{1,0:T(8,128)}, f32[64,4096]{1,0:T(8,128)S(1)}, u32[]{:S(2)}) %copy-start) | copy-done | bytes 1048600
  85.6 0.0 copy-start.1
  85.6 0.6 copy-done.1
  86.2 3.1 %finish.1 = (f32[64,4096]{1,0:T(8,128)}, f32[2,4,8]{2,1,0:T(4,128)}, f32[4,8]{1,0:T(4,128)}) custom-call(f32[1,384]{1,0:T(1,128)} %copy-done.1, f32[64,4096]{1,0:T(8,128)} %copy-done), custom_call_target="tpu_custom_call" | custom-call | tf_op jit(solution)/shard_map/finish/pallas_call | solution.py:492
Async XLA Ops:
  84.7 1.0 %copy-start = (f32[64,4096]{1,0:T(8,128)}, f32[64,4096]{1,0:T(8,128)S(1)}, u32[]{:S(2)}) copy-start(f32[64,4096]{1,0:T(8,128)S(1)} %get-tuple-element.9.scaled) | copy-start | bytes 3145732
  85.6 0.6 copy-start.1

commit v3 on v2

--- a/solution.py
+++ b/solution.py
@@ -32,16 +32,15 @@
     surf, area, mask, tarea, tiles_in, tile_of, block_of, live_in,
     scaled, tot_out,
     surf_v, ext, am_v, mask_v, ta_v, w_v, idx, sm, s_acc, reach_sum, psend, prec,
-    s_msg, rxm, msg, rx, rxw, run, rxp,
+    s_msg, rs0, rxm, msg, rx, mid, rxw, run, rxp,
     lsem, ssem, isend, irecv, msend, mrecv, dsend, drecv, wsend, wrecv, csend, crecv,
-    pssem, prsem, upper_in, lower_in, mem_in,
+    pssem, prsem, zsend, zrecv, hsend, upper_in, mem_in,
 ):
     columns, own, tgt, slots, tiles, members, reach = shape
     me = lax.axis_index("band")
     my_mem = lax.axis_index("mem")
     has_low = me > 0
     has_up = me < n - 1
-    half = n // 2
 
     def band(o):
         return {"band": me + o}
@@ -58,18 +57,22 @@
     def tell(sem, where):
         pl.semaphore_signal(sem, inc=1, device_id=where, device_id_type=MESH)
 
+    stride = n // 8
+    last = n - n // 4
     barrier = pltpu.get_barrier_semaphore()
 
-    @pl.when(has_low)
-    def _():
-        tell(barrier, band(-1))
-
-    @pl.when(has_up)
-    def _():
-        tell(barrier, band(1))
-
-    for where in (mem(1), mem(mems - 1)):
-        tell(barrier, where)
+    def tell_band(q, carry):
+        tell(barrier, {"band": q})
+        return carry
+
+    lax.fori_loop(me + 1, jnp.where(me == 0, stride + 1, n), tell_band, 0)
+    lax.fori_loop(jnp.where(me == 0, last, n), n, tell_band, 0)
+
+    def tell_mem(m, carry):
+        tell(barrier, {"mem": m})
+        return carry
+
+    lax.fori_loop(jnp.where(has_low, my_mem + 1, mems), mems, tell_mem, 0)
 
     loads = [
         pltpu.make_async_copy(block_of, idx.at[0, 0:slots], lsem.at[0]),
@@ -90,13 +93,15 @@
         )
         for q in range(parts)
     ]
-    for c in loads[:5] + pieces[:2] + loads[5:] + pieces[2:]:
+    for c in loads[:5] + pieces + loads[5:]:
         c.start()
     w_v[tiles] = jnp.zeros((128, 128), BF16)
-    for c in loads[:3]:
-        c.wait()
     scalars = [pltpu.make_async_copy(idx.at[i], sm.at[i], lsem.at[i]) for i in range(3)]
-    scalars[0].start()
+
+    def own_lists():
+        for c in loads[:3]:
+            c.wait()
+        scalars[0].start()
 
     def weigh(s, total):
         at = pl.ds(pl.multiple_of(s * 128, 128), 128)
@@ -115,7 +120,6 @@
         s_acc[...] = total
         loads[5].wait()
         loads[6].wait()
-        scalars[0].wait()
 
     def slot_sum(which, t, shift, alive):
         live = sm[which, 2 * slots, t] * alive
@@ -143,56 +147,78 @@
 
         lax.fori_loop(0, tgt, body, 0)
 
-    @pl.when(me == 0)
-    def _():
+    early = has_low & (me <= stride)
+
+    @pl.when(early)
+    def _():
+        own_lists()
         local_part()
+        scalars[0].wait()
         own_targets()
 
-    near = has_low.astype(I32) + has_up.astype(I32)
-    pl.semaphore_wait(barrier, near + 2)
+    known = me - 1 + ((me <= stride) | (me >= last)).astype(I32)
+
+    @pl.when(has_low)
+    def _():
+        pl.semaphore_wait(barrier, known + my_mem)
+
+    for o in range(1, stride + 1):
+        @pl.when(me >= o)
+        def _():
+            tell(upper_in.at[o - 1], band(-o))
+
+    def tell_mem_back(m, carry):
+        tell(mem_in.at[my_mem], {"mem": m})
+        return carry
+
+    lax.fori_loop(0, jnp.where(has_low, my_mem, 0), tell_mem_back, 0)
+
+    pl.when(jnp.logical_not(early))(own_lists)
     to_low = remote(idx.at[0], idx.at[2], isend.at[0], irecv.at[0], band(-1))
     to_up = remote(idx.at[0], idx.at[1], isend.at[1], irecv.at[1], band(1))
 
     @pl.when(has_low)
     def _():
         to_low.start()
-        tell(upper_in, band(-1))
 
     @pl.when(has_up)
     def _():
+        pl.semaphore_wait(upper_in.at[0], 1)
         to_up.start()
 
-    for where in (mem(1), mem(mems - 1)):
-        tell(mem_in, where)
-
-    @pl.when(me > 1)
-    def _():
-        pl.semaphore_wait(lower_in, 1)
-
-    @pl.when((me > 0) & has_up)
-    def _():
-        tell(lower_in, band(1))
-
-    @pl.when(has_low)
-    def _():
-        local_part()
-
-    @pl.when(has_low & (me < half))
-    def _():
-        own_targets()
+    pl.when(jnp.logical_not(early))(local_part)
 
     ones = jnp.ones((8, 128), F32)
     s_row = row_dot(ones, s_acc[...], HIGHEST)[0:1]
     s_msg[...] = jnp.concatenate([s_row, jnp.zeros((1, 128 - columns), F32)], axis=1)
 
+    first_row = remote(s_msg, rs0, zsend, zrecv, band(1))
+    pl.when(me == 0)(first_row.start)
+
+    @pl.when(me == 1)
+    def _():
+        first_row.wait_recv()
+        s_msg[...] = s_msg[...] + rs0[...]
+
+    def from_mem(m, to):
+        return remote(s_msg, rxm.at[m], msend.at[to], mrecv.at[m], {"mem": to})
+
+    def others(action):
+        for m in range(mems):
+            pl.when(has_low & (my_mem != m))(functools.partial(action, m))
+
+    def send_mem(m):
+        @pl.when(my_mem < m)
+        def _():
+            pl.semaphore_wait(mem_in.at[m], 1)
+
+        from_mem(my_mem, m).start()
+
+    others(send_mem)
+
     flat_w = w_v[0:tiles].reshape(tiles * 128, 128)
     sums = row_dot(jnp.ones((8, 128), BF16), flat_w)
     row_sums = jnp.concatenate([sums[0:1, q * 128 : (q + 1) * 128] for q in range(tiles)], axis=0)
-
-    pl.semaphore_wait(mem_in, 2)
-    to_mem = [remote(s_msg, rxm.at[my_mem], msend.at[d], mrecv.at[my_mem], mem(d)) for d in range(1, mems)]
-    for c in to_mem:
-        c.start()
 
     place = lax.broadcasted_iota(I32, (slots, tgt), 0)
     lane = lax.broadcasted_iota(I32, (slots, tgt), 1)
@@ -203,24 +229,6 @@
         alive = place < idx[i, 2 * slots : 2 * slots + 1, :]
         return block, jnp.where(alive, tile, -1)
 
-    def cell_sums(block, tile):
-        count = slots * tgt
-        block_row = jnp.concatenate([block[k : k + 1] for k in range(slots)], axis=1)
-        tile_row = jnp.concatenate([tile[k : k + 1] for k in range(slots)], axis=1)
-        at_block = (lax.broadcasted_iota(I32, (own, count), 0) == block_row).astype(F32).astype(BF16)
-        at_tile = (lax.broadcasted_iota(I32, (tiles, count), 0) == tile_row).astype(F32).astype(BF16)
-        return lax.dot_general(
-            row_dot(at_block, at_tile), row_sums, (((1,), (0,)), ((), ())),
-            preferred_element_type=F32, precision=HIGHEST,
-        )
-
-    def weigh_target(s, total):
-        return total + ext[s].astype(F32) * reach_sum[pl.ds(s, 1), :]
-
-    b0, w0 = listed(0)
-    reach_sum[...] = cell_sums(b0 - HALO, w0)
-    t_acc = lax.fori_loop(0, own, weigh_target, jnp.zeros((columns, 128), F32), unroll=4)
-
     @pl.when(has_low)
     def _():
         to_up.wait_recv()
@@ -231,22 +239,31 @@
         to_low.wait_recv()
         scalars[2].start()
 
+    b0, w0 = listed(0)
     b1, w1 = listed(1)
     b2, w2 = listed(2)
     from_low = (lane >= tgt - reach) & has_low
     from_up = (lane < reach) & has_up
-    reach_sum[...] = cell_sums(
-        jnp.where(from_low, b1 - (HALO + own), b2 - HALO + own),
-        jnp.where(from_low, w1, jnp.where(from_up, w2, -1)),
-    )
-    t_acc = lax.fori_loop(0, HALO, weigh_target, t_acc, unroll=4)
-    t_acc = lax.fori_loop(own - HALO, own, weigh_target, t_acc, unroll=4)
+    pair_b = (b0 - HALO, jnp.where(from_low, b1 - (HALO + own), b2 - HALO + own))
+    pair_w = (w0, jnp.where(from_low, w1, jnp.where(from_up, w2, -1)))
+    count = 2 * slots * tgt
+    block_row = jnp.concatenate([x[k : k + 1] for x in pair_b for k in range(slots)], axis=1)
+    tile_row = jnp.concatenate([x[k : k + 1] for x in pair_w for k in range(slots)], axis=1)
+    at_block = (lax.broadcasted_iota(I32, (own, count), 0) == block_row).astype(F32).astype(BF16)
+    at_tile = (lax.broadcasted_iota(I32, (tiles, count), 0) == tile_row).astype(F32).astype(BF16)
+    reach_sum[...] = lax.dot_general(
+        row_dot(at_block, at_tile), row_sums, (((1,), (0,)), ((), ())),
+        preferred_element_type=F32, precision=HIGHEST,
+    )
+
+    def weigh_target(s, total):
+        return total + ext[s].astype(F32) * reach_sum[pl.ds(s, 1), :]
+
+    t_acc = lax.fori_loop(0, own, weigh_target, jnp.zeros((columns, 128), F32), unroll=4)
     t_row = row_dot(ones, t_acc, HIGHEST)[0:1]
 
     rxm[my_mem] = s_msg[...]
-    for d in range(1, mems):
-        other = lax.rem(my_mem + d, mems)
-        remote(s_msg, rxm.at[other], msend.at[d], mrecv.at[other], mem(d)).wait_recv()
+    others(lambda m: from_mem(m, m).wait_recv())
     e_row = rxm[0]
     for m in range(1, mems):
         e_row = e_row + rxm[m]
@@ -254,6 +271,7 @@
     e_sum = e_row[:, 0:per]
     for m in range(1, members):
         e_sum = e_sum + e_row[:, m * per : (m + 1) * per]
+    e_sum = jnp.where(has_low, e_sum, 0.0)
     a_sum = jnp.sum(jnp.sum(ta_v[...], axis=0, keepdims=True), axis=1, keepdims=True)
     a_high = jnp.round(a_sum * 64.0) * (1.0 / 64.0)
     s_parts, e_parts = in_three(s_row), in_three(e_sum)
@@ -271,29 +289,19 @@
         direct(q).start()
         return carry
 
-    lax.fori_loop(0, me, send_down, 0)
-
-    stride = n // 8
-
-    @pl.when(has_up)
-    def _():
-        for _ in range(stride - 2):
-            pl.semaphore_wait(upper_in, 1)
-
-            @pl.when(has_low)
-            def _():
-                tell(upper_in, band(-1))
-
-        pl.semaphore_wait(upper_in, 1)
-
-    @pl.when(me == n - 1)
-    def _():
-        for _ in range(stride - 2):
-            tell(upper_in, band(-1))
+    lowest = jnp.where((me == 1) | (me >= last), 0, 1)
+    lax.fori_loop(lowest, me, send_down, 0)
+
+    for o in range(2, stride + 1):
+        @pl.when(me + o < n)
+        def _():
+            pl.semaphore_wait(upper_in.at[o - 1], 1)
 
     ups = [remote(msg, rxw.at[o - 1], wsend.at[o - 1], wrecv.at[o - 1], band(o)) for o in range(1, stride)]
     for o, c in enumerate(ups, 1):
         pl.when(me + o < n)(c.start)
+
+    pl.when(jnp.logical_not(early))(scalars[0].wait)
 
     @pl.when(has_low)
     def _():
@@ -328,9 +336,7 @@
     pl.when(has_low)(functools.partial(for_side, 0))
     pl.when(has_up)(functools.partial(for_side, 1))
 
-    @pl.when(me >= half)
-    def _():
-        own_targets()
+    pl.when(jnp.logical_not(early))(own_targets)
 
     def add_part(side, start):
         def body(i, carry):
@@ -367,21 +373,31 @@
     pl.when(me + stride < n)(chain.start)
 
     def add_upper(q, total):
-        remote(msg, rx.at[q], dsend.at[0], drecv.at[q], {"band": q}).wait_recv()
+        remote(msg, rx.at[q], dsend.at[q], drecv.at[q], {"band": q}).wait_recv()
         return total + rx[q]
 
-    tot_out[...] = lax.fori_loop(me + 1, n, add_upper, run[...])
+    is_first = me == 0
+    between = lax.fori_loop(
+        jnp.where(is_first, n, me + 1), jnp.where(me < last, last, me + 1), add_upper,
+        jnp.zeros((1, WORDS), F32),
+    )
+    mid[...] = between
+    hand = remote(mid, rx.at[2], hsend, drecv.at[2], band(-1))
+    pl.when(me == 1)(hand.start)
+    total = lax.fori_loop(1, jnp.where(is_first, 3, 1), add_upper, run[...] + between)
+    tot_out[...] = lax.fori_loop(jnp.maximum(me + 1, last), n, add_upper, total)
 
     def sent(q, carry):
         direct(q).wait_send()
         return carry
 
-    lax.fori_loop(0, me, sent, 0)
+    lax.fori_loop(lowest, me, sent, 0)
+    pl.when(me == 0)(first_row.wait_send)
+    pl.when(me == 1)(hand.wait_send)
     pl.when(me + stride < n)(chain.wait_send)
     for o, c in enumerate(ups, 1):
         pl.when(me + o < n)(c.wait_send)
-    for c in to_mem:
-        c.wait_send()
+    others(lambda m: from_mem(my_mem, m).wait_send())
 
     def parts_sent(side):
         def body(i, carry):
@@ -401,7 +417,7 @@
         parts_sent(1)
 
 
-def last_kernel(shape, mems, tot, scaled, out, conserved, ensemble, done, sems):
+def last_kernel(shape, mems, tot, scaled, out, conserved, ensemble, done, mean_v, group_v, sems):
     columns, members, fields, snaps = shape
     per = columns // members
 
@@ -417,21 +433,26 @@
         I32, (columns, columns), 1
     )
     fix = jnp.broadcast_to(jnp.sum(jnp.where(diagonal, step, 0.0), axis=1, keepdims=True), (columns, 128))
-    pieces = 4
-    width = out.shape[1] // pieces
-    copies = []
-    for q in range(pieces):
-        for b in range(q * width // 128, (q + 1) * width // 128):
-            done[:, b * 128 : (b + 1) * 128] = scaled[:, b * 128 : (b + 1) * 128] + fix
-        where = (slice(None), slice(q * width, (q + 1) * width))
-        copies.append(pltpu.make_async_copy(done.at[where], out.at[where], sems.at[q]))
-        copies[-1].start()
     mean = s / total_area
     for i in range(members * fields):
-        conserved[i // fields, i % fields : i % fields + 1, :] = mean[:, i * snaps : (i + 1) * snaps]
+        mean_v[i // fields, i % fields : i % fields + 1, :] = mean[:, i * snaps : (i + 1) * snaps]
     group = e / total_area / float(members * mems)
     for f in range(fields):
-        ensemble[f : f + 1, :] = group[:, f * snaps : (f + 1) * snaps]
+        group_v[f : f + 1, :] = group[:, f * snaps : (f + 1) * snaps]
+    pieces = 4
+    copies = [
+        pltpu.make_async_copy(mean_v, conserved, sems.at[pieces]),
+        pltpu.make_async_copy(group_v, ensemble, sems.at[pieces + 1]),
+    ]
+    for q in range(pieces):
+        rows = slice(q * columns // pieces, (q + 1) * columns // pieces)
+        for b in range(out.shape[1] // 128):
+            done[rows, b * 128 : (b + 1) * 128] = scaled[rows, b * 128 : (b + 1) * 128] + fix[rows]
+        copies.append(pltpu.make_async_copy(done.at[rows], out.at[rows], sems.at[q]))
+        copies[-1].start()
+        if q == 0:
+            copies[0].start()
+            copies[1].start()
     for c in copies:
         c.wait()
 
@@ -466,15 +487,17 @@
             pltpu.VMEM((2, reach, columns, 128), F32),
             pltpu.VMEM((2, reach, columns, 128), F32),
             pltpu.VMEM((1, 128), F32),
+            pltpu.VMEM((1, 128), F32),
             pltpu.VMEM((mems, 1, 128), F32),
             pltpu.VMEM((1, WORDS), F32),
             pltpu.VMEM((n, 1, WORDS), F32),
+            pltpu.VMEM((1, WORDS), F32),
             pltpu.VMEM((stride - 1, 1, WORDS), F32),
             pltpu.VMEM((1, WORDS), F32),
             pltpu.VMEM((1, WORDS), F32),
             dma((7,)), dma((4,)), dma((2,)), dma((2,)), dma((mems,)), dma((mems,)),
             dma((n,)), dma((n,)), dma((stride - 1,)), dma((stride - 1,)), dma, dma,
-            dma((2, reach)), dma((2, reach)), plain, plain, plain,
+            dma((2, reach)), dma((2, reach)), dma, dma, dma, plain((stride,)), plain((mems,)),
         ],
         compiler_params=pltpu.CompilerParams(collective_id=0, has_side_effects=True),
         name="regrid",
@@ -497,8 +520,14 @@
             jax.ShapeDtypeStruct((fields, snaps), F32),
         ),
         in_specs=[inside, inside],
-        out_specs=(any_space, inside, inside),
-        scratch_shapes=[pltpu.VMEM((columns, tgt * 128), F32), dma((4,))],
+        out_specs=(any_space,) * 3,
+        scratch_shapes=[
+            pltpu.VMEM((columns, tgt * 128), F32),
+            pltpu.VMEM((members, fields, snaps), F32),
+            pltpu.VMEM((fields, snaps), F32),
+            dma((6,)),
+        ],
+        compiler_params=pltpu.CompilerParams(vmem_limit_bytes=8 * 2**20),
         name="finish",
     )(tot, scaled)
     return out.reshape(members, fields, snaps, tgt * 128), conserved, ensemble

time: 89.5 us -> 65.6 us (0.73)
  Pallas kernels: 87.1 us -> 64.8 us
  local copies, waits for them, and re-layouts: 1.55 us -> 0 us
    pallas_call x1, Pallas kernels: 84 us -> 63.5 us  [on_device(): pl.pallas_call(functools.partial(main_kernel, n, mems, (columns, own, tgt...]
    pallas_call x1, Pallas kernels: 3.11 us -> 1.29 us  [on_device(): pl.pallas_call(functools.partial(last_kernel, (columns, members, fields,...]
    unnamed x4 -> x0, local copies, waits for them, and re-layouts: 1.55 us -> none
where the time goes in v3:
time: 65.6 us; the launch traced here: 65.4 us
  Pallas kernels  64.8 us (99%)
    pallas_call x1, Pallas kernels, on_device(): pl.pallas_call(functools.partial(main_kernel, n, mems, (columns, own, tgt...  63.5 us

profile of v3, /device:TPU:34, one launch (start us, length us, event | category | flops | bytes accessed | tf_op | source)
XLA Modules:
  0.0 65.4 jit_solution(17808753839559111438)
XLA Ops:
  0.6 63.5 %regrid.1 = (f32[64,4096]{1,0:T(8,128)S(1)}, f32[1,384]{1,0:T(1,128)S(1)}) custom-call(bf16[64,16384]{1,0:T(8,128)(2,1)} %bitcast.8, f32[128,128]{1,0:T(8,128)} %bitcast.9, s32[128,128]{1,0:T(8,128)} %bitcast.10, f32[32,128]{1,0:T(8,128)} %bitcast.11, bf16[16,128,128]{2,1,0:T(8,128)(2,1)} %tiles_in.1, s32[24,32]{1,0:T(8,128)} %bitcast.12, ...), custom_call_target="tpu_custom_call" | custom-call | tf_op jit(solution)/shard_map/regrid/pallas_call | solution.py:471
  64.1 1.3 %finish.1 = (f32[64,4096]{1,0:T(8,128)}, f32[2,4,8]{2,1,0:T(4,128)}, f32[4,8]{1,0:T(4,128)}) custom-call(f32[1,384]{1,0:T(1,128)S(1)} %get-tuple-element.8.tot, f32[64,4096]{1,0:T(8,128)S(1)} %get-tuple-element.9.scaled), custom_call_target="tpu_custom_call" | custom-call | tf_op jit(solution)/shard_map/finish/pallas_call | solution.py:515

commit v4 on v3

--- a/solution.py
+++ b/solution.py
@@ -31,8 +31,8 @@
     n, mems, shape,
     surf, area, mask, tarea, tiles_in, tile_of, block_of, live_in,
     scaled, tot_out,
-    surf_v, ext, am_v, mask_v, ta_v, w_v, idx, sm, s_acc, reach_sum, psend, prec,
-    s_msg, rs0, rxm, msg, rx, mid, rxw, run, rxp,
+    surf_v, ext, am_v, mask_v, ta_v, w_v, idx, packed, told, local, sm, s_acc, reach_sum, psend, prec,
+    s_msg, rs0, rxm, msg, msg_up, rx0, rx, mid, rxw, run, rxp,
     lsem, ssem, isend, irecv, msend, mrecv, dsend, drecv, wsend, wrecv, csend, crecv,
     pssem, prsem, zsend, zrecv, hsend, upper_in, mem_in,
 ):
@@ -41,12 +41,13 @@
     my_mem = lax.axis_index("mem")
     has_low = me > 0
     has_up = me < n - 1
+    stride = n // 8
+    last = n - n // 8
+    early = has_low & (me <= stride)
+    late = jnp.logical_not(early)
 
     def band(o):
         return {"band": me + o}
-
-    def mem(o):
-        return {"mem": lax.rem(my_mem + o, mems)}
 
     def remote(src, dst, send, recv, where):
         return pltpu.make_async_remote_copy(
@@ -57,15 +58,13 @@
     def tell(sem, where):
         pl.semaphore_signal(sem, inc=1, device_id=where, device_id_type=MESH)
 
-    stride = n // 8
-    last = n - n // 4
     barrier = pltpu.get_barrier_semaphore()
 
     def tell_band(q, carry):
         tell(barrier, {"band": q})
         return carry
 
-    lax.fori_loop(me + 1, jnp.where(me == 0, stride + 1, n), tell_band, 0)
+    lax.fori_loop(me + 1, jnp.where(me == 0, 2, n), tell_band, 0)
     lax.fori_loop(jnp.where(me == 0, last, n), n, tell_band, 0)
 
     def tell_mem(m, carry):
@@ -75,9 +74,9 @@
     lax.fori_loop(jnp.where(has_low, my_mem + 1, mems), mems, tell_mem, 0)
 
     loads = [
-        pltpu.make_async_copy(block_of, idx.at[0, 0:slots], lsem.at[0]),
-        pltpu.make_async_copy(tile_of, idx.at[0, slots : 2 * slots], lsem.at[1]),
-        pltpu.make_async_copy(live_in, idx.at[0, 2 * slots : 2 * slots + 1], lsem.at[2]),
+        pltpu.make_async_copy(block_of, idx.at[0:slots], lsem.at[0]),
+        pltpu.make_async_copy(tile_of, idx.at[slots : 2 * slots], lsem.at[1]),
+        pltpu.make_async_copy(live_in, idx.at[2 * slots : 2 * slots + 1], lsem.at[2]),
         pltpu.make_async_copy(area, am_v, lsem.at[3]),
         pltpu.make_async_copy(mask, mask_v, lsem.at[4]),
         pltpu.make_async_copy(tiles_in, w_v.at[0:tiles], lsem.at[5]),
@@ -96,11 +95,24 @@
     for c in loads[:5] + pieces + loads[5:]:
         c.start()
     w_v[tiles] = jnp.zeros((128, 128), BF16)
-    scalars = [pltpu.make_async_copy(idx.at[i], sm.at[i], lsem.at[i]) for i in range(3)]
+
+    place = lax.broadcasted_iota(I32, (slots, tgt), 0)
+    lane = lax.broadcasted_iota(I32, (slots, tgt), 1)
+    scalars = [pltpu.make_async_copy(local.at[i], sm.at[i], lsem.at[i]) for i in range(3)]
+
+    def make_local(i, word, shift, valid):
+        block = (word & 255) + shift
+        good = valid & (block >= 0) & (block < own)
+        tile = jnp.where(good, word >> 8, tiles)
+        local[i] = jnp.clip(block, 0, own - 1) + 256 * tile
 
     def own_lists():
         for c in loads[:3]:
             c.wait()
+        alive = place < idx[2 * slots : 2 * slots + 1, :]
+        word = idx[0:slots, :] + 256 * jnp.where(alive, idx[slots : 2 * slots, :], tiles)
+        packed[...] = word
+        make_local(0, word, -HALO, alive)
         scalars[0].start()
 
     def weigh(s, total):
@@ -121,16 +133,14 @@
         loads[5].wait()
         loads[6].wait()
 
-    def slot_sum(which, t, shift, alive):
-        live = sm[which, 2 * slots, t] * alive
+    def slot_sum(which, t):
         total = None
         for p in range(slots // 2):
             left, right = [], []
             for k in (2 * p, 2 * p + 1):
-                block = sm[which, k, t] + shift
-                good = (k < live) & (block >= 0) & (block < own)
-                left.append(ext[jnp.clip(block, 0, own - 1)])
-                right.append(w_v[jnp.where(good, sm[which, slots + k, t], tiles)])
+                word = sm[which, k, t]
+                left.append(ext[word & 255])
+                right.append(w_v[word >> 8])
             term = jnp.dot(
                 jnp.concatenate(left, axis=1), jnp.concatenate(right, axis=0), preferred_element_type=F32
             )
@@ -142,12 +152,10 @@
 
     def own_targets():
         def body(t, carry):
-            scaled[:, columns_of(t)] = slot_sum(0, t, -HALO, 1)
+            scaled[:, columns_of(t)] = slot_sum(0, t)
             return carry
 
         lax.fori_loop(0, tgt, body, 0)
-
-    early = has_low & (me <= stride)
 
     @pl.when(early)
     def _():
@@ -156,16 +164,15 @@
         scalars[0].wait()
         own_targets()
 
-    known = me - 1 + ((me <= stride) | (me >= last)).astype(I32)
+    known = me - 1 + ((me == 1) | (me >= last)).astype(I32)
 
     @pl.when(has_low)
     def _():
         pl.semaphore_wait(barrier, known + my_mem)
 
-    for o in range(1, stride + 1):
-        @pl.when(me >= o)
-        def _():
-            tell(upper_in.at[o - 1], band(-o))
+    pl.when(has_low)(lambda: tell(upper_in.at[0], band(-1)))
+    for o in range(2, stride + 1):
+        pl.when(me > o)(functools.partial(tell, upper_in.at[o - 1], band(-o)))
 
     def tell_mem_back(m, carry):
         tell(mem_in.at[my_mem], {"mem": m})
@@ -173,26 +180,23 @@
 
     lax.fori_loop(0, jnp.where(has_low, my_mem, 0), tell_mem_back, 0)
 
-    pl.when(jnp.logical_not(early))(own_lists)
-    to_low = remote(idx.at[0], idx.at[2], isend.at[0], irecv.at[0], band(-1))
-    to_up = remote(idx.at[0], idx.at[1], isend.at[1], irecv.at[1], band(1))
-
-    @pl.when(has_low)
-    def _():
-        to_low.start()
+    pl.when(late)(own_lists)
+    to_low = remote(packed, told.at[1], isend.at[0], irecv.at[0], band(-1))
+    to_up = remote(packed, told.at[0], isend.at[1], irecv.at[1], band(1))
+    pl.when(has_low)(to_low.start)
 
     @pl.when(has_up)
     def _():
         pl.semaphore_wait(upper_in.at[0], 1)
         to_up.start()
 
-    pl.when(jnp.logical_not(early))(local_part)
+    pl.when(late)(local_part)
 
     ones = jnp.ones((8, 128), F32)
     s_row = row_dot(ones, s_acc[...], HIGHEST)[0:1]
     s_msg[...] = jnp.concatenate([s_row, jnp.zeros((1, 128 - columns), F32)], axis=1)
 
-    first_row = remote(s_msg, rs0, zsend, zrecv, band(1))
+    first_row = remote(s_msg, rs0, zsend.at[0], zrecv.at[0], band(1))
     pl.when(me == 0)(first_row.start)
 
     @pl.when(me == 1)
@@ -203,67 +207,82 @@
     def from_mem(m, to):
         return remote(s_msg, rxm.at[m], msend.at[to], mrecv.at[m], {"mem": to})
 
-    def others(action):
+    def others(action, which):
         for m in range(mems):
-            pl.when(has_low & (my_mem != m))(functools.partial(action, m))
-
-    def send_mem(m):
-        @pl.when(my_mem < m)
-        def _():
-            pl.semaphore_wait(mem_in.at[m], 1)
-
-        from_mem(my_mem, m).start()
-
-    others(send_mem)
+            pl.when(has_low & which(m))(functools.partial(action, m))
+
+    others(lambda m: from_mem(my_mem, m).start(), lambda m: my_mem > m)
 
     flat_w = w_v[0:tiles].reshape(tiles * 128, 128)
     sums = row_dot(jnp.ones((8, 128), BF16), flat_w)
     row_sums = jnp.concatenate([sums[0:1, q * 128 : (q + 1) * 128] for q in range(tiles)], axis=0)
 
-    place = lax.broadcasted_iota(I32, (slots, tgt), 0)
-    lane = lax.broadcasted_iota(I32, (slots, tgt), 1)
-
-    def listed(i):
-        block = idx[i, 0:slots, :]
-        tile = idx[i, slots : 2 * slots, :]
-        alive = place < idx[i, 2 * slots : 2 * slots + 1, :]
-        return block, jnp.where(alive, tile, -1)
-
-    @pl.when(has_low)
-    def _():
-        to_up.wait_recv()
-        scalars[1].start()
-
-    @pl.when(has_up)
-    def _():
-        to_low.wait_recv()
-        scalars[2].start()
-
-    b0, w0 = listed(0)
-    b1, w1 = listed(1)
-    b2, w2 = listed(2)
+    def cell_sums(word):
+        row = jnp.concatenate([word[k : k + 1] for k in range(slots)], axis=1)
+        count = slots * tgt
+        at_block = (lax.broadcasted_iota(I32, (own, count), 0) == (row & 255)).astype(F32).astype(BF16)
+        at_tile = (lax.broadcasted_iota(I32, (tiles, count), 0) == (row >> 8)).astype(F32).astype(BF16)
+        return lax.dot_general(
+            row_dot(at_block, at_tile), row_sums, (((1,), (0,)), ((), ())),
+            preferred_element_type=F32, precision=HIGHEST,
+        )
+
+    def weigh_target(s, total):
+        return total + ext[s].astype(F32) * reach_sum[pl.ds(s, 1), :]
+
+    reach_sum[...] = cell_sums(local[0])
+    t_acc = lax.fori_loop(0, own, weigh_target, jnp.zeros((columns, 128), F32), unroll=4)
+
+    pl.when(has_low)(to_up.wait_recv)
+    pl.when(has_up)(to_low.wait_recv)
+
+    def send_higher(m):
+        pl.semaphore_wait(mem_in.at[m], 1)
+        from_mem(my_mem, m).start()
+
+    others(send_higher, lambda m: my_mem < m)
+
     from_low = (lane >= tgt - reach) & has_low
     from_up = (lane < reach) & has_up
-    pair_b = (b0 - HALO, jnp.where(from_low, b1 - (HALO + own), b2 - HALO + own))
-    pair_w = (w0, jnp.where(from_low, w1, jnp.where(from_up, w2, -1)))
-    count = 2 * slots * tgt
-    block_row = jnp.concatenate([x[k : k + 1] for x in pair_b for k in range(slots)], axis=1)
-    tile_row = jnp.concatenate([x[k : k + 1] for x in pair_w for k in range(slots)], axis=1)
-    at_block = (lax.broadcasted_iota(I32, (own, count), 0) == block_row).astype(F32).astype(BF16)
-    at_tile = (lax.broadcasted_iota(I32, (tiles, count), 0) == tile_row).astype(F32).astype(BF16)
-    reach_sum[...] = lax.dot_general(
-        row_dot(at_block, at_tile), row_sums, (((1,), (0,)), ((), ())),
-        preferred_element_type=F32, precision=HIGHEST,
-    )
-
-    def weigh_target(s, total):
-        return total + ext[s].astype(F32) * reach_sum[pl.ds(s, 1), :]
-
-    t_acc = lax.fori_loop(0, own, weigh_target, jnp.zeros((columns, 128), F32), unroll=4)
+    make_local(1, told[0], -(HALO + own), from_low)
+    make_local(2, told[1], own - HALO, from_up)
+    reach_sum[...] = cell_sums(jnp.where(lane < reach, local[2], local[1]))
+    t_acc = lax.fori_loop(0, HALO, weigh_target, t_acc, unroll=4)
+    t_acc = lax.fori_loop(own - HALO, own, weigh_target, t_acc, unroll=4)
     t_row = row_dot(ones, t_acc, HIGHEST)[0:1]
+    scalars[1].start()
+    scalars[2].start()
+
+    def part_copy(side, i):
+        return remote(
+            psend.at[side, i], prec.at[1 - side, i], pssem.at[side, i], prsem.at[1 - side, i],
+            band(2 * side - 1),
+        )
+
+    def for_side(side):
+        def body(i, carry):
+            psend[side, i] = slot_sum(1 + side, i + (tgt - reach if side == 0 else 0))
+
+            @pl.when(i > 0)
+            def _():
+                part_copy(side, i - 1).start()
+
+            return carry
+
+        lax.fori_loop(0, reach, body, 0)
+        part_copy(side, reach - 1).start()
+
+    def for_neighbours():
+        pl.when(late)(scalars[0].wait)
+        scalars[1].wait()
+        scalars[2].wait()
+        pl.when(has_low)(functools.partial(for_side, 0))
+        pl.when(has_up)(functools.partial(for_side, 1))
+
+    pl.when(me == 1)(for_neighbours)
 
     rxm[my_mem] = s_msg[...]
-    others(lambda m: from_mem(m, m).wait_recv())
+    others(lambda m: from_mem(m, m).wait_recv(), lambda m: my_mem != m)
     e_row = rxm[0]
     for m in range(1, mems):
         e_row = e_row + rxm[m]
@@ -292,51 +311,34 @@
     lowest = jnp.where((me == 1) | (me >= last), 0, 1)
     lax.fori_loop(lowest, me, send_down, 0)
 
-    for o in range(2, stride + 1):
-        @pl.when(me + o < n)
-        def _():
+    from_first = remote(msg, rx0, zsend.at[1], zrecv.at[1], band(1))
+
+    pl.when(me == 0)(from_first.start)
+
+    msg_up[...] = msg[...]
+
+    @pl.when(me == 1)
+    def _():
+        from_first.wait_recv()
+        msg_up[...] = msg[...] + rx0[...]
+
+    ups = [remote(msg_up, rxw.at[o - 1], wsend.at[o - 1], wrecv.at[o - 1], band(o)) for o in range(1, stride)]
+    chain = remote(run, rxp, csend, crecv, band(stride))
+
+    def to_higher(o):
+        return has_low & (me + o < n)
+
+    def send_up(o):
+        if o > 1:
             pl.semaphore_wait(upper_in.at[o - 1], 1)
-
-    ups = [remote(msg, rxw.at[o - 1], wsend.at[o - 1], wrecv.at[o - 1], band(o)) for o in range(1, stride)]
-    for o, c in enumerate(ups, 1):
-        pl.when(me + o < n)(c.start)
-
-    pl.when(jnp.logical_not(early))(scalars[0].wait)
-
-    @pl.when(has_low)
-    def _():
-        scalars[1].wait()
-
-    @pl.when(has_up)
-    def _():
-        scalars[2].wait()
-
-    def part_copy(side, i):
-        return remote(
-            psend.at[side, i], prec.at[1 - side, i], pssem.at[side, i], prsem.at[1 - side, i],
-            band(2 * side - 1),
-        )
-
-    def for_side(side):
-        def body(i, carry):
-            if side == 0:
-                psend[0, i] = slot_sum(1, tgt - reach + i, -(HALO + own), 1)
-            else:
-                psend[1, i] = slot_sum(2, i, own - HALO, 1)
-
-            @pl.when(i > 0)
-            def _():
-                part_copy(side, i - 1).start()
-
-            return carry
-
-        lax.fori_loop(0, reach, body, 0)
-        part_copy(side, reach - 1).start()
-
-    pl.when(has_low)(functools.partial(for_side, 0))
-    pl.when(has_up)(functools.partial(for_side, 1))
-
-    pl.when(jnp.logical_not(early))(own_targets)
+        if o < stride:
+            ups[o - 1].start()
+
+    for o in range(1, stride + 1):
+        pl.when(to_higher(o))(functools.partial(send_up, o))
+
+    pl.when(me != 1)(for_neighbours)
+    pl.when(late)(own_targets)
 
     def add_part(side, start):
         def body(i, carry):
@@ -356,21 +358,21 @@
     pl.when(has_up)(functools.partial(add_part, 1, tgt - reach))
     lax.fori_loop(0, tgt, divide, 0)
 
-    run[...] = msg[...]
-    for o, c in enumerate(ups, 1):
-        @pl.when(me >= o)
-        def _():
-            c.wait_recv()
-            run[...] = run[...] + rxw[o - 1]
-
-    chain = remote(run, rxp, csend, crecv, band(stride))
-
-    @pl.when(me >= stride)
+    run[...] = msg_up[...]
+
+    def add_window(o):
+        ups[o - 1].wait_recv()
+        run[...] = run[...] + rxw[o - 1]
+
+    for o in range(1, stride):
+        pl.when(me > o)(functools.partial(add_window, o))
+
+    @pl.when(me > stride)
     def _():
         chain.wait_recv()
         run[...] = run[...] + rxp[...]
 
-    pl.when(me + stride < n)(chain.start)
+    pl.when(to_higher(stride))(chain.start)
 
     def add_upper(q, total):
         remote(msg, rx.at[q], dsend.at[q], drecv.at[q], {"band": q}).wait_recv()
@@ -392,12 +394,16 @@
         return carry
 
     lax.fori_loop(lowest, me, sent, 0)
-    pl.when(me == 0)(first_row.wait_send)
+    @pl.when(me == 0)
+    def _():
+        first_row.wait_send()
+        from_first.wait_send()
+
     pl.when(me == 1)(hand.wait_send)
-    pl.when(me + stride < n)(chain.wait_send)
-    for o, c in enumerate(ups, 1):
-        pl.when(me + o < n)(c.wait_send)
-    others(lambda m: from_mem(my_mem, m).wait_send())
+    pl.when(to_higher(stride))(chain.wait_send)
+    for o in range(1, stride):
+        pl.when(to_higher(o))(ups[o - 1].wait_send)
+    others(lambda m: from_mem(my_mem, m).wait_send(), lambda m: my_mem != m)
 
     def parts_sent(side):
         def body(i, carry):
@@ -480,8 +486,11 @@
             pltpu.VMEM((own, 128), I32),
             pltpu.VMEM((tgt, 128), F32),
             pltpu.VMEM((tiles + 1, 128, 128), BF16),
-            pltpu.VMEM((3, rows, tgt), I32),
-            pltpu.SMEM((3, rows, tgt), I32),
+            pltpu.VMEM((rows, tgt), I32),
+            pltpu.VMEM((slots, tgt), I32),
+            pltpu.VMEM((2, slots, tgt), I32),
+            pltpu.VMEM((3, slots, tgt), I32),
+            pltpu.SMEM((3, slots, tgt), I32),
             pltpu.VMEM((columns, 128), F32),
             pltpu.VMEM((own, 128), F32),
             pltpu.VMEM((2, reach, columns, 128), F32),
@@ -490,6 +499,8 @@
             pltpu.VMEM((1, 128), F32),
             pltpu.VMEM((mems, 1, 128), F32),
             pltpu.VMEM((1, WORDS), F32),
+            pltpu.VMEM((1, WORDS), F32),
+            pltpu.VMEM((1, WORDS), F32),
             pltpu.VMEM((n, 1, WORDS), F32),
             pltpu.VMEM((1, WORDS), F32),
             pltpu.VMEM((stride - 1, 1, WORDS), F32),
@@ -497,7 +508,7 @@
             pltpu.VMEM((1, WORDS), F32),
             dma((7,)), dma((4,)), dma((2,)), dma((2,)), dma((mems,)), dma((mems,)),
             dma((n,)), dma((n,)), dma((stride - 1,)), dma((stride - 1,)), dma, dma,
-            dma((2, reach)), dma((2, reach)), dma, dma, dma, plain((stride,)), plain((mems,)),
+            dma((2, reach)), dma((2, reach)), dma((2,)), dma((2,)), dma, plain((stride,)), plain((mems,)),
         ],
         compiler_params=pltpu.CompilerParams(collective_id=0, has_side_effects=True),
         name="regrid",

time: 65.6 us -> 61.7 us (0.941)
  Pallas kernels: 64.8 us -> 60.9 us
    pallas_call x1, Pallas kernels: 63.5 us -> 59.6 us  [on_device(): pl.pallas_call(functools.partial(main_kernel, n, mems, (columns, own, tgt...]
where the time goes in v4:
time: 61.7 us; the launch traced here: 61.6 us
  Pallas kernels  60.9 us (99%)
  between operations  0.64 us (1%)
    pallas_call x1, Pallas kernels, on_device(): pl.pallas_call(functools.partial(main_kernel, n, mems, (columns, own, tgt...  59.6 us
    pallas_call x1, Pallas kernels, on_device(): pl.pallas_call(functools.partial(last_kernel, (columns, members, fields,...  1.29 us

profile of v4, /device:TPU:34, one launch (start us, length us, event | category | flops | bytes accessed | tf_op | source)
XLA Modules:
  0.0 61.6 jit_solution(9319741169271636336)
XLA Ops:
  0.6 59.6 %regrid.1 = (f32[64,4096]{1,0:T(8,128)S(1)}, f32[1,384]{1,0:T(1,128)S(1)}) custom-call(bf16[64,16384]{1,0:T(8,128)(2,1)} %bitcast.8, f32[128,128]{1,0:T(8,128)} %bitcast.9, s32[128,128]{1,0:T(8,128)} %bitcast.10, f32[32,128]{1,0:T(8,128)} %bitcast.11, bf16[16,128,128]{2,1,0:T(8,128)(2,1)} %tiles_in.1, s32[24,32]{1,0:T(8,128)} %bitcast.12, ...), custom_call_target="tpu_custom_call" | custom-call | tf_op jit(solution)/shard_map/regrid/pallas_call | solution.py:477
  60.3 1.3 %finish.1 = (f32[64,4096]{1,0:T(8,128)}, f32[2,4,8]{2,1,0:T(4,128)}, f32[4,8]{1,0:T(4,128)}) custom-call(f32[1,384]{1,0:T(1,128)S(1)} %get-tuple-element.8.tot, f32[64,4096]{1,0:T(8,128)S(1)} %get-tuple-element.9.scaled), custom_call_target="tpu_custom_call" | custom-call | tf_op jit(solution)/shard_map/finish/pallas_call | solution.py:526

commit v5 on v4

--- a/solution.py
+++ b/solution.py
@@ -42,7 +42,8 @@
     has_low = me > 0
     has_up = me < n - 1
     stride = n // 8
-    last = n - n // 8
+    via = (lax.axis_index("grp") == 0) & (my_mem == 0) & (lax.axis_index("fld") == 0)
+    last = jnp.where(via, n, 2)
     early = has_low & (me <= stride)
     late = jnp.logical_not(early)
 
@@ -185,11 +186,6 @@
     to_up = remote(packed, told.at[0], isend.at[1], irecv.at[1], band(1))
     pl.when(has_low)(to_low.start)
 
-    @pl.when(has_up)
-    def _():
-        pl.semaphore_wait(upper_in.at[0], 1)
-        to_up.start()
-
     pl.when(late)(local_part)
 
     ones = jnp.ones((8, 128), F32)
@@ -197,7 +193,12 @@
     s_msg[...] = jnp.concatenate([s_row, jnp.zeros((1, 128 - columns), F32)], axis=1)
 
     first_row = remote(s_msg, rs0, zsend.at[0], zrecv.at[0], band(1))
-    pl.when(me == 0)(first_row.start)
+
+    @pl.when(me == 0)
+    def _():
+        pl.semaphore_wait(upper_in.at[0], 1)
+        first_row.start()
+
 
     @pl.when(me == 1)
     def _():
@@ -216,6 +217,12 @@
     flat_w = w_v[0:tiles].reshape(tiles * 128, 128)
     sums = row_dot(jnp.ones((8, 128), BF16), flat_w)
     row_sums = jnp.concatenate([sums[0:1, q * 128 : (q + 1) * 128] for q in range(tiles)], axis=0)
+
+    @pl.when(has_low & has_up)
+    def _():
+        pl.semaphore_wait(upper_in.at[0], 1)
+
+    pl.when(has_up)(to_up.start)
 
     def cell_sums(word):
         row = jnp.concatenate([word[k : k + 1] for k in range(slots)], axis=1)
@@ -253,9 +260,12 @@
     scalars[1].start()
     scalars[2].start()
 
-    def part_copy(side, i):
+    chunk = 2
+
+    def part_copy(side, j):
+        at = pl.ds(chunk * j, chunk)
         return remote(
-            psend.at[side, i], prec.at[1 - side, i], pssem.at[side, i], prsem.at[1 - side, i],
+            psend.at[side, at], prec.at[1 - side, at], pssem.at[side, j], prsem.at[1 - side, j],
             band(2 * side - 1),
         )
 
@@ -263,14 +273,14 @@
         def body(i, carry):
             psend[side, i] = slot_sum(1 + side, i + (tgt - reach if side == 0 else 0))
 
-            @pl.when(i > 0)
+            @pl.when((i > 0) & (lax.rem(i, chunk) == 0))
             def _():
-                part_copy(side, i - 1).start()
+                part_copy(side, lax.div(i, chunk) - 1).start()
 
             return carry
 
         lax.fori_loop(0, reach, body, 0)
-        part_copy(side, reach - 1).start()
+        part_copy(side, reach // chunk - 1).start()
 
     def for_neighbours():
         pl.when(late)(scalars[0].wait)
@@ -301,14 +311,23 @@
         axis=1,
     )
 
+    group, ways = 4, 8
+
     def direct(q):
-        return remote(msg, rx.at[me], dsend.at[q], drecv.at[me], {"band": q})
+        return remote(
+            msg, rx.at[me], dsend.at[lax.rem(q, ways)], drecv.at[lax.div(me, group)], {"band": q}
+        )
+
+    lowest = jnp.where((me == 1) | (me >= last), 0, 1)
 
     def send_down(q, carry):
+        @pl.when(q - ways >= lowest)
+        def _():
+            direct(q - ways).wait_send()
+
         direct(q).start()
         return carry
 
-    lowest = jnp.where((me == 1) | (me >= last), 0, 1)
     lax.fori_loop(lowest, me, send_down, 0)
 
     from_first = remote(msg, rx0, zsend.at[1], zrecv.at[1], band(1))
@@ -341,13 +360,14 @@
     pl.when(late)(own_targets)
 
     def add_part(side, start):
-        def body(i, carry):
-            part_copy(1 - side, i).wait_recv()
-            at = columns_of(start + i)
-            scaled[:, at] = scaled[:, at] + prec[side, i]
+        def body(j, carry):
+            part_copy(1 - side, j).wait_recv()
+            for i in range(chunk):
+                at = columns_of(start + chunk * j + i)
+                scaled[:, at] = scaled[:, at] + prec[side, chunk * j + i]
             return carry
 
-        lax.fori_loop(0, reach, body, 0)
+        lax.fori_loop(0, reach // chunk, body, 0)
 
     def divide(t, carry):
         at = columns_of(t)
@@ -374,43 +394,25 @@
 
     pl.when(to_higher(stride))(chain.start)
 
-    def add_upper(q, total):
-        remote(msg, rx.at[q], dsend.at[q], drecv.at[q], {"band": q}).wait_recv()
-        return total + rx[q]
-
-    is_first = me == 0
-    between = lax.fori_loop(
-        jnp.where(is_first, n, me + 1), jnp.where(me < last, last, me + 1), add_upper,
-        jnp.zeros((1, WORDS), F32),
-    )
-    mid[...] = between
-    hand = remote(mid, rx.at[2], hsend, drecv.at[2], band(-1))
-    pl.when(me == 1)(hand.start)
-    total = lax.fori_loop(1, jnp.where(is_first, 3, 1), add_upper, run[...] + between)
-    tot_out[...] = lax.fori_loop(jnp.maximum(me + 1, last), n, add_upper, total)
-
     def sent(q, carry):
         direct(q).wait_send()
         return carry
 
-    lax.fori_loop(lowest, me, sent, 0)
+    lax.fori_loop(jnp.maximum(lowest, me - ways), me, sent, 0)
+
     @pl.when(me == 0)
     def _():
         first_row.wait_send()
         from_first.wait_send()
 
-    pl.when(me == 1)(hand.wait_send)
     pl.when(to_higher(stride))(chain.wait_send)
     for o in range(1, stride):
         pl.when(to_higher(o))(ups[o - 1].wait_send)
     others(lambda m: from_mem(my_mem, m).wait_send(), lambda m: my_mem != m)
 
     def parts_sent(side):
-        def body(i, carry):
-            part_copy(side, i).wait_send()
-            return carry
-
-        lax.fori_loop(0, reach, body, 0)
+        for j in range(reach // chunk):
+            part_copy(side, j).wait_send()
 
     @pl.when(has_low)
     def _():
@@ -421,6 +423,29 @@
     def _():
         to_up.wait_send()
         parts_sent(1)
+
+    def arrived(start, count, g):
+        at = rx.at[pl.ds(start, count)]
+        remote(at, at, dsend.at[0], drecv.at[g], {"band": lax.rem(me + 1, n)}).wait_recv()
+        for i in range(count):
+            mid[...] = mid[...] + rx[start + i]
+
+    mine = lax.div(me, group)
+    near = jnp.where(via & (me == 0), 2, group - 1 - lax.rem(me, group))
+    mid[...] = jnp.zeros((1, WORDS), F32)
+    for count in range(1, group):
+        pl.when(near == count)(functools.partial(arrived, me + 1, count, mine))
+
+    def add_group(g, carry):
+        arrived(group * g, group, g)
+        return carry
+
+    lax.fori_loop(jnp.where(via & (me == 0), n // group, mine + 1), n // group, add_group, 0)
+
+    hand = remote(mid, rx.at[2], hsend, drecv.at[0], band(-1))
+    pl.when(via & (me == 1))(hand.start)
+    tot_out[...] = run[...] + mid[...]
+    pl.when(via & (me == 1))(hand.wait_send)
 
 
 def last_kernel(shape, mems, tot, scaled, out, conserved, ensemble, done, mean_v, group_v, sems):
@@ -507,8 +532,8 @@
             pltpu.VMEM((1, WORDS), F32),
             pltpu.VMEM((1, WORDS), F32),
             dma((7,)), dma((4,)), dma((2,)), dma((2,)), dma((mems,)), dma((mems,)),
-            dma((n,)), dma((n,)), dma((stride - 1,)), dma((stride - 1,)), dma, dma,
-            dma((2, reach)), dma((2, reach)), dma((2,)), dma((2,)), dma, plain((stride,)), plain((mems,)),
+            dma((8,)), dma((n // 4,)), dma((stride - 1,)), dma((stride - 1,)), dma, dma,
+            dma((2, reach // 2)), dma((2, reach // 2)), dma((2,)), dma((2,)), dma, plain((stride,)), plain((mems,)),
         ],
         compiler_params=pltpu.CompilerParams(collective_id=0, has_side_effects=True),
         name="regrid",

time: 61.7 us -> 60.6 us (0.982)
  the two profiles are of different devices: /device:TPU:34 before, /device:TPU:96 now
where the time goes in v5:
time: 60.6 us; the launch traced here: 60.5 us
  Pallas kernels  59.8 us (99%)
  between operations  0.64 us (1%)
    pallas_call x1, Pallas kernels, on_device(): pl.pallas_call(functools.partial(main_kernel, n, mems, (columns, own, tgt...  58.5 us
    pallas_call x1, Pallas kernels, on_device(): pl.pallas_call(functools.partial(last_kernel, (columns, members, fields,...  1.29 us

profile of v5, /device:TPU:96, one launch (start us, length us, event | category | flops | bytes accessed | tf_op | source)
XLA Modules:
  0.0 60.5 jit_solution(8078257950561104314)
XLA Ops:
  0.6 58.5 %regrid.1 = (f32[64,4096]{1,0:T(8,128)S(1)}, f32[1,384]{1,0:T(1,128)S(1)}) custom-call(bf16[64,16384]{1,0:T(8,128)(2,1)} %bitcast.8, f32[128,128]{1,0:T(8,128)} %bitcast.9, s32[128,128]{1,0:T(8,128)} %bitcast.10, f32[32,128]{1,0:T(8,128)} %bitcast.11, bf16[16,128,128]{2,1,0:T(8,128)(2,1)} %tiles_in.1, s32[24,32]{1,0:T(8,128)} %bitcast.12, ...), custom_call_target="tpu_custom_call" | custom-call | tf_op jit(solution)/shard_map/regrid/pallas_call | solution.py:502
  59.2 1.3 %finish.1 = (f32[64,4096]{1,0:T(8,128)}, f32[2,4,8]{2,1,0:T(4,128)}, f32[4,8]{1,0:T(4,128)}) custom-call(f32[1,384]{1,0:T(1,128)S(1)} %get-tuple-element.8.tot, f32[64,4096]{1,0:T(8,128)S(1)} %get-tuple-element.9.scaled), custom_call_target="tpu_custom_call" | custom-call | tf_op jit(solution)/shard_map/finish/pallas_call | solution.py:551

commit v6 on v5

--- a/solution.py
+++ b/solution.py
@@ -186,6 +186,11 @@
     to_up = remote(packed, told.at[0], isend.at[1], irecv.at[1], band(1))
     pl.when(has_low)(to_low.start)
 
+    def send_list_up():
+        pl.semaphore_wait(upper_in.at[0], 1)
+        to_up.start()
+
+    pl.when(early)(send_list_up)
     pl.when(late)(local_part)
 
     ones = jnp.ones((8, 128), F32)
@@ -196,14 +201,8 @@
 
     @pl.when(me == 0)
     def _():
-        pl.semaphore_wait(upper_in.at[0], 1)
+        send_list_up()
         first_row.start()
-
-
-    @pl.when(me == 1)
-    def _():
-        first_row.wait_recv()
-        s_msg[...] = s_msg[...] + rs0[...]
 
     def from_mem(m, to):
         return remote(s_msg, rxm.at[m], msend.at[to], mrecv.at[m], {"mem": to})
@@ -212,17 +211,16 @@
         for m in range(mems):
             pl.when(has_low & which(m))(functools.partial(action, m))
 
-    others(lambda m: from_mem(my_mem, m).start(), lambda m: my_mem > m)
+    def send_lower(m):
+        from_mem(my_mem, m).start()
+
+    others(send_lower, lambda m: (my_mem > m) & (me > 1))
 
     flat_w = w_v[0:tiles].reshape(tiles * 128, 128)
     sums = row_dot(jnp.ones((8, 128), BF16), flat_w)
     row_sums = jnp.concatenate([sums[0:1, q * 128 : (q + 1) * 128] for q in range(tiles)], axis=0)
 
-    @pl.when(has_low & has_up)
-    def _():
-        pl.semaphore_wait(upper_in.at[0], 1)
-
-    pl.when(has_up)(to_up.start)
+    pl.when(late & has_low & has_up)(send_list_up)
 
     def cell_sums(word):
         row = jnp.concatenate([word[k : k + 1] for k in range(slots)], axis=1)
@@ -240,6 +238,12 @@
     reach_sum[...] = cell_sums(local[0])
     t_acc = lax.fori_loop(0, own, weigh_target, jnp.zeros((columns, 128), F32), unroll=4)
 
+    @pl.when(me == 1)
+    def _():
+        first_row.wait_recv()
+        s_msg[...] = s_msg[...] + rs0[...]
+
+    others(send_lower, lambda m: (my_mem > m) & (me == 1))
     pl.when(has_low)(to_up.wait_recv)
     pl.when(has_up)(to_low.wait_recv)
 
@@ -283,13 +287,12 @@
         part_copy(side, reach // chunk - 1).start()
 
     def for_neighbours():
-        pl.when(late)(scalars[0].wait)
         scalars[1].wait()
         scalars[2].wait()
         pl.when(has_low)(functools.partial(for_side, 0))
         pl.when(has_up)(functools.partial(for_side, 1))
 
-    pl.when(me == 1)(for_neighbours)
+    pl.when(early)(for_neighbours)
 
     rxm[my_mem] = s_msg[...]
     others(lambda m: from_mem(m, m).wait_recv(), lambda m: my_mem != m)
@@ -356,8 +359,28 @@
     for o in range(1, stride + 1):
         pl.when(to_higher(o))(functools.partial(send_up, o))
 
-    pl.when(me != 1)(for_neighbours)
-    pl.when(late)(own_targets)
+    pl.when(late)(for_neighbours)
+    @pl.when(late)
+    def _():
+        scalars[0].wait()
+        own_targets()
+
+
+    run[...] = msg_up[...]
+
+    def add_window(o):
+        ups[o - 1].wait_recv()
+        run[...] = run[...] + rxw[o - 1]
+
+    for o in range(1, stride):
+        pl.when(me > o)(functools.partial(add_window, o))
+
+    @pl.when(me > stride)
+    def _():
+        chain.wait_recv()
+        run[...] = run[...] + rxp[...]
+
+    pl.when(to_higher(stride))(chain.start)
 
     def add_part(side, start):
         def body(j, carry):
@@ -377,22 +400,6 @@
     pl.when(has_low)(functools.partial(add_part, 0, 0))
     pl.when(has_up)(functools.partial(add_part, 1, tgt - reach))
     lax.fori_loop(0, tgt, divide, 0)
-
-    run[...] = msg_up[...]
-
-    def add_window(o):
-        ups[o - 1].wait_recv()
-        run[...] = run[...] + rxw[o - 1]
-
-    for o in range(1, stride):
-        pl.when(me > o)(functools.partial(add_window, o))
-
-    @pl.when(me > stride)
-    def _():
-        chain.wait_recv()
-        run[...] = run[...] + rxp[...]
-
-    pl.when(to_higher(stride))(chain.start)
 
     def sent(q, carry):
         direct(q).wait_send()

time: 60.6 us -> 59 us (0.974)
  Pallas kernels: 59.8 us -> 58.2 us
    pallas_call x1, Pallas kernels: 58.5 us -> 56.9 us  [on_device(): pl.pallas_call(functools.partial(main_kernel, n, mems, (columns, own, tgt...]
where the time goes in v6:
time: 59 us; the launch traced here: 58.8 us
  Pallas kernels  58.2 us (99%)
  between operations  0.64 us (1%)
    pallas_call x1, Pallas kernels, on_device(): pl.pallas_call(functools.partial(main_kernel, n, mems, (columns, own, tgt...  56.9 us
    pallas_call x1, Pallas kernels, on_device(): pl.pallas_call(functools.partial(last_kernel, (columns, members, fields,...  1.29 us

profile of v6, /device:TPU:96, one launch (start us, length us, event | category | flops | bytes accessed | tf_op | source)
XLA Modules:
  0.0 58.8 jit_solution(5364049018691833586)
XLA Ops:
  0.6 56.9 %regrid.1 = (f32[64,4096]{1,0:T(8,128)S(1)}, f32[1,384]{1,0:T(1,128)S(1)}) custom-call(bf16[64,16384]{1,0:T(8,128)(2,1)} %bitcast.8, f32[128,128]{1,0:T(8,128)} %bitcast.9, s32[128,128]{1,0:T(8,128)} %bitcast.10, f32[32,128]{1,0:T(8,128)} %bitcast.11, bf16[16,128,128]{2,1,0:T(8,128)(2,1)} %tiles_in.1, s32[24,32]{1,0:T(8,128)} %bitcast.12, ...), custom_call_target="tpu_custom_call" | custom-call | tf_op jit(solution)/shard_map/regrid/pallas_call | solution.py:509
  57.5 1.3 %finish.1 = (f32[64,4096]{1,0:T(8,128)}, f32[2,4,8]{2,1,0:T(4,128)}, f32[4,8]{1,0:T(4,128)}) custom-call(f32[1,384]{1,0:T(1,128)S(1)} %get-tuple-element.8.tot, f32[64,4096]{1,0:T(8,128)S(1)} %get-tuple-element.9.scaled), custom_call_target="tpu_custom_call" | custom-call | tf_op jit(solution)/shard_map/finish/pallas_call | solution.py:558

commit v7 on v6

--- a/solution.py
+++ b/solution.py
@@ -32,9 +32,9 @@
     surf, area, mask, tarea, tiles_in, tile_of, block_of, live_in,
     scaled, tot_out,
     surf_v, ext, am_v, mask_v, ta_v, w_v, idx, packed, told, local, sm, s_acc, reach_sum, psend, prec,
-    s_msg, rs0, rxm, msg, msg_up, rx0, rx, mid, rxw, run, rxp,
+    s_msg, rs0, rxm, msg, msg_up, rx0, rx, mid, rxw, run, rxp, rtot,
     lsem, ssem, isend, irecv, msend, mrecv, dsend, drecv, wsend, wrecv, csend, crecv,
-    pssem, prsem, zsend, zrecv, hsend, upper_in, mem_in,
+    pssem, prsem, zsend, zrecv, hsend, tsend, trecv, upper_in, mem_in, want,
 ):
     columns, own, tgt, slots, tiles, members, reach = shape
     me = lax.axis_index("band")
@@ -44,6 +44,9 @@
     stride = n // 8
     via = (lax.axis_index("grp") == 0) & (my_mem == 0) & (lax.axis_index("fld") == 0)
     last = jnp.where(via, n, 2)
+    first = n // 4
+    fan = 4
+    is_first = me <= first
     early = has_low & (me <= stride)
     late = jnp.logical_not(early)
 
@@ -173,7 +176,13 @@
 
     pl.when(has_low)(lambda: tell(upper_in.at[0], band(-1)))
     for o in range(2, stride + 1):
-        pl.when(me > o)(functools.partial(tell, upper_in.at[o - 1], band(-o)))
+        pl.when((me > o) & is_first)(functools.partial(tell, upper_in.at[o - 1], band(-o)))
+
+    def ask():
+        back = me - first - 1
+        tell(want.at[lax.div(back, fan)], {"band": first + 1 - fan + lax.rem(back, fan)})
+
+    pl.when(jnp.logical_not(is_first))(ask)
 
     def tell_mem_back(m, carry):
         tell(mem_in.at[my_mem], {"mem": m})
@@ -292,7 +301,8 @@
         pl.when(has_low)(functools.partial(for_side, 0))
         pl.when(has_up)(functools.partial(for_side, 1))
 
-    pl.when(early)(for_neighbours)
+    parts_first = early & jnp.logical_not(via)
+    pl.when(parts_first)(for_neighbours)
 
     rxm[my_mem] = s_msg[...]
     others(lambda m: from_mem(m, m).wait_recv(), lambda m: my_mem != m)
@@ -314,24 +324,19 @@
         axis=1,
     )
 
-    group, ways = 4, 8
+    group = 4
 
     def direct(q):
-        return remote(
-            msg, rx.at[me], dsend.at[lax.rem(q, ways)], drecv.at[lax.div(me, group)], {"band": q}
-        )
+        return remote(msg, rx.at[me], dsend.at[q], drecv.at[lax.div(me, group)], {"band": q})
 
     lowest = jnp.where((me == 1) | (me >= last), 0, 1)
+    highest = jnp.minimum(me, first + 1)
 
     def send_down(q, carry):
-        @pl.when(q - ways >= lowest)
-        def _():
-            direct(q - ways).wait_send()
-
         direct(q).start()
         return carry
 
-    lax.fori_loop(lowest, me, send_down, 0)
+    lax.fori_loop(lowest, highest, send_down, 0)
 
     from_first = remote(msg, rx0, zsend.at[1], zrecv.at[1], band(1))
 
@@ -348,7 +353,7 @@
     chain = remote(run, rxp, csend, crecv, band(stride))
 
     def to_higher(o):
-        return has_low & (me + o < n)
+        return has_low & (me + o <= first)
 
     def send_up(o):
         if o > 1:
@@ -359,7 +364,7 @@
     for o in range(1, stride + 1):
         pl.when(to_higher(o))(functools.partial(send_up, o))
 
-    pl.when(late)(for_neighbours)
+    pl.when(jnp.logical_not(parts_first))(for_neighbours)
     @pl.when(late)
     def _():
         scalars[0].wait()
@@ -373,9 +378,9 @@
         run[...] = run[...] + rxw[o - 1]
 
     for o in range(1, stride):
-        pl.when(me > o)(functools.partial(add_window, o))
-
-    @pl.when(me > stride)
+        pl.when((me > o) & is_first)(functools.partial(add_window, o))
+
+    @pl.when((me > stride) & is_first)
     def _():
         chain.wait_recv()
         run[...] = run[...] + rxp[...]
@@ -405,7 +410,7 @@
         direct(q).wait_send()
         return carry
 
-    lax.fori_loop(jnp.maximum(lowest, me - ways), me, sent, 0)
+    lax.fori_loop(lowest, highest, sent, 0)
 
     @pl.when(me == 0)
     def _():
@@ -441,17 +446,42 @@
     near = jnp.where(via & (me == 0), 2, group - 1 - lax.rem(me, group))
     mid[...] = jnp.zeros((1, WORDS), F32)
     for count in range(1, group):
-        pl.when(near == count)(functools.partial(arrived, me + 1, count, mine))
+        pl.when(is_first & (near == count))(functools.partial(arrived, me + 1, count, mine))
 
     def add_group(g, carry):
         arrived(group * g, group, g)
         return carry
 
-    lax.fori_loop(jnp.where(via & (me == 0), n // group, mine + 1), n // group, add_group, 0)
+    no_more = (via & (me == 0)) | jnp.logical_not(is_first)
+    lax.fori_loop(jnp.where(no_more, n // group, mine + 1), n // group, add_group, 0)
 
     hand = remote(mid, rx.at[2], hsend, drecv.at[0], band(-1))
     pl.when(via & (me == 1))(hand.start)
-    tot_out[...] = run[...] + mid[...]
+    run[...] = run[...] + mid[...]
+
+    def total_to(k):
+        return remote(run, rtot, tsend.at[k], trecv, band(fan * (k + 1)))
+
+    def give(k):
+        pl.semaphore_wait(want.at[k], 1)
+        total_to(k).start()
+
+    count = -(-(n - first - 1) // fan)
+    gives = [is_first & (me > first - fan) & (me + fan * (k + 1) < n) for k in range(count)]
+    for k in range(count):
+        pl.when(gives[k])(functools.partial(give, k))
+
+    @pl.when(is_first)
+    def _():
+        tot_out[...] = run[...]
+
+    @pl.when(jnp.logical_not(is_first))
+    def _():
+        remote(run, rtot, tsend.at[0], trecv, band(-1)).wait_recv()
+        tot_out[...] = rtot[...]
+
+    for k in range(count):
+        pl.when(gives[k])(total_to(k).wait_send)
     pl.when(via & (me == 1))(hand.wait_send)
 
 
@@ -538,9 +568,11 @@
             pltpu.VMEM((stride - 1, 1, WORDS), F32),
             pltpu.VMEM((1, WORDS), F32),
             pltpu.VMEM((1, WORDS), F32),
+            pltpu.VMEM((1, WORDS), F32),
             dma((7,)), dma((4,)), dma((2,)), dma((2,)), dma((mems,)), dma((mems,)),
-            dma((8,)), dma((n // 4,)), dma((stride - 1,)), dma((stride - 1,)), dma, dma,
-            dma((2, reach // 2)), dma((2, reach // 2)), dma((2,)), dma((2,)), dma, plain((stride,)), plain((mems,)),
+            dma((n // 4 + 1,)), dma((n // 4,)), dma((stride - 1,)), dma((stride - 1,)), dma, dma,
+            dma((2, reach // 2)), dma((2, reach // 2)), dma((2,)), dma((2,)), dma,
+            dma((n // 4,)), dma, plain((stride,)), plain((mems,)), plain((n // 4,)),
         ],
         compiler_params=pltpu.CompilerParams(collective_id=0, has_side_effects=True),
         name="regrid",

time: 59 us -> 58.4 us (0.990)
  Pallas kernels: 58.2 us -> 57.6 us
    pallas_call x1, Pallas kernels: 56.9 us -> 56.3 us  [on_device(): pl.pallas_call(functools.partial(main_kernel, n, mems, (columns, own, tgt...]
where the time goes in v7:
time: 58.4 us; the launch traced here: 58.2 us
  Pallas kernels  57.6 us (99%)
  between operations  0.64 us (1%)
    pallas_call x1, Pallas kernels, on_device(): pl.pallas_call(functools.partial(main_kernel, n, mems, (columns, own, tgt...  56.3 us
    pallas_call x1, Pallas kernels, on_device(): pl.pallas_call(functools.partial(last_kernel, (columns, members, fields,...  1.29 us

profile of v7, /device:TPU:96, one launch (start us, length us, event | category | flops | bytes accessed | tf_op | source)
XLA Modules:
  0.0 58.2 jit_solution(8655002724906092624)
XLA Ops:
  0.6 56.3 %regrid.1 = (f32[64,4096]{1,0:T(8,128)S(1)}, f32[1,384]{1,0:T(1,128)S(1)}) custom-call(bf16[64,16384]{1,0:T(8,128)(2,1)} %bitcast.8, f32[128,128]{1,0:T(8,128)} %bitcast.9, s32[128,128]{1,0:T(8,128)} %bitcast.10, f32[32,128]{1,0:T(8,128)} %bitcast.11, bf16[16,128,128]{2,1,0:T(8,128)(2,1)} %tiles_in.1, s32[24,32]{1,0:T(8,128)} %bitcast.12, ...), custom_call_target="tpu_custom_call" | custom-call | tf_op jit(solution)/shard_map/regrid/pallas_call | solution.py:539
  56.9 1.3 %finish.1 = (f32[64,4096]{1,0:T(8,128)}, f32[2,4,8]{2,1,0:T(4,128)}, f32[4,8]{1,0:T(4,128)}) custom-call(f32[1,384]{1,0:T(1,128)S(1)} %get-tuple-element.8.tot, f32[64,4096]{1,0:T(8,128)S(1)} %get-tuple-element.9.scaled), custom_call_target="tpu_custom_call" | custom-call | tf_op jit(solution)/shard_map/finish/pallas_call | solution.py:590

commit v8 on v7

--- a/solution.py
+++ b/solution.py
@@ -32,8 +32,8 @@
     surf, area, mask, tarea, tiles_in, tile_of, block_of, live_in,
     scaled, tot_out,
     surf_v, ext, am_v, mask_v, ta_v, w_v, idx, packed, told, local, sm, s_acc, reach_sum, psend, prec,
-    s_msg, rs0, rxm, msg, msg_up, rx0, rx, mid, rxw, run, rxp, rtot,
-    lsem, ssem, isend, irecv, msend, mrecv, dsend, drecv, wsend, wrecv, csend, crecv,
+    s_msg, rs0, rxm, msg, msg_up, rx0, rx, mid, rxw, run, rtot,
+    lsem, ssem, isend, irecv, msend, mrecv, dsend, drecv, wsend, wrecv,
     pssem, prsem, zsend, zrecv, hsend, tsend, trecv, upper_in, mem_in, want,
 ):
     columns, own, tgt, slots, tiles, members, reach = shape
@@ -44,8 +44,8 @@
     stride = n // 8
     via = (lax.axis_index("grp") == 0) & (my_mem == 0) & (lax.axis_index("fld") == 0)
     last = jnp.where(via, n, 2)
-    first = n // 4
-    fan = 4
+    first = stride
+    fan = 2
     is_first = me <= first
     early = has_low & (me <= stride)
     late = jnp.logical_not(early)
@@ -175,12 +175,12 @@
         pl.semaphore_wait(barrier, known + my_mem)
 
     pl.when(has_low)(lambda: tell(upper_in.at[0], band(-1)))
-    for o in range(2, stride + 1):
+    for o in range(2, stride):
         pl.when((me > o) & is_first)(functools.partial(tell, upper_in.at[o - 1], band(-o)))
 
     def ask():
         back = me - first - 1
-        tell(want.at[lax.div(back, fan)], {"band": first + 1 - fan + lax.rem(back, fan)})
+        tell(want, {"band": first + 1 - fan + lax.rem(back, fan)})
 
     pl.when(jnp.logical_not(is_first))(ask)
 
@@ -342,6 +342,8 @@
 
     pl.when(me == 0)(from_first.start)
 
+    pl.when(jnp.logical_not(parts_first))(for_neighbours)
+
     msg_up[...] = msg[...]
 
     @pl.when(me == 1)
@@ -350,7 +352,6 @@
         msg_up[...] = msg[...] + rx0[...]
 
     ups = [remote(msg_up, rxw.at[o - 1], wsend.at[o - 1], wrecv.at[o - 1], band(o)) for o in range(1, stride)]
-    chain = remote(run, rxp, csend, crecv, band(stride))
 
     def to_higher(o):
         return has_low & (me + o <= first)
@@ -358,13 +359,11 @@
     def send_up(o):
         if o > 1:
             pl.semaphore_wait(upper_in.at[o - 1], 1)
-        if o < stride:
-            ups[o - 1].start()
-
-    for o in range(1, stride + 1):
+        ups[o - 1].start()
+
+    for o in range(1, stride):
         pl.when(to_higher(o))(functools.partial(send_up, o))
 
-    pl.when(jnp.logical_not(parts_first))(for_neighbours)
     @pl.when(late)
     def _():
         scalars[0].wait()
@@ -379,13 +378,6 @@
 
     for o in range(1, stride):
         pl.when((me > o) & is_first)(functools.partial(add_window, o))
-
-    @pl.when((me > stride) & is_first)
-    def _():
-        chain.wait_recv()
-        run[...] = run[...] + rxp[...]
-
-    pl.when(to_higher(stride))(chain.start)
 
     def add_part(side, start):
         def body(j, carry):
@@ -417,7 +409,6 @@
         first_row.wait_send()
         from_first.wait_send()
 
-    pl.when(to_higher(stride))(chain.wait_send)
     for o in range(1, stride):
         pl.when(to_higher(o))(ups[o - 1].wait_send)
     others(lambda m: from_mem(my_mem, m).wait_send(), lambda m: my_mem != m)
@@ -459,17 +450,18 @@
     pl.when(via & (me == 1))(hand.start)
     run[...] = run[...] + mid[...]
 
-    def total_to(k):
-        return remote(run, rtot, tsend.at[k], trecv, band(fan * (k + 1)))
-
-    def give(k):
-        pl.semaphore_wait(want.at[k], 1)
-        total_to(k).start()
-
-    count = -(-(n - first - 1) // fan)
-    gives = [is_first & (me > first - fan) & (me + fan * (k + 1) < n) for k in range(count)]
-    for k in range(count):
-        pl.when(gives[k])(functools.partial(give, k))
+    def total_to(p, words, to):
+        return remote(words, to, tsend, trecv, {"band": p})
+
+    def give(count):
+        pl.semaphore_wait(want, count)
+        for k in range(count):
+            total_to(me + fan * (k + 1), run, rtot).start()
+
+    rest = n - first - 1
+    gives = [(me == first + 1 - fan + r, len(range(r, rest, fan))) for r in range(fan)]
+    for mine_to_give, count in gives:
+        pl.when(mine_to_give)(functools.partial(give, count))
 
     @pl.when(is_first)
     def _():
@@ -477,11 +469,11 @@
 
     @pl.when(jnp.logical_not(is_first))
     def _():
-        remote(run, rtot, tsend.at[0], trecv, band(-1)).wait_recv()
+        total_to(me - 1, run, rtot).wait_recv()
         tot_out[...] = rtot[...]
 
-    for k in range(count):
-        pl.when(gives[k])(total_to(k).wait_send)
+    for mine_to_give, count in gives:
+        pl.when(mine_to_give)(total_to(me + 1, rx.at[0:count], rx.at[0:count]).wait_send)
     pl.when(via & (me == 1))(hand.wait_send)
 
 
@@ -568,11 +560,10 @@
             pltpu.VMEM((stride - 1, 1, WORDS), F32),
             pltpu.VMEM((1, WORDS), F32),
             pltpu.VMEM((1, WORDS), F32),
-            pltpu.VMEM((1, WORDS), F32),
             dma((7,)), dma((4,)), dma((2,)), dma((2,)), dma((mems,)), dma((mems,)),
-            dma((n // 4 + 1,)), dma((n // 4,)), dma((stride - 1,)), dma((stride - 1,)), dma, dma,
+            dma((stride + 1,)), dma((n // 4,)), dma((stride - 1,)), dma((stride - 1,)),
             dma((2, reach // 2)), dma((2, reach // 2)), dma((2,)), dma((2,)), dma,
-            dma((n // 4,)), dma, plain((stride,)), plain((mems,)), plain((n // 4,)),
+            dma, dma, plain((stride - 1,)), plain((mems,)), plain,
         ],
         compiler_params=pltpu.CompilerParams(collective_id=0, has_side_effects=True),
         name="regrid",

time: 58.4 us -> 57.3 us (0.981)
  Pallas kernels: 57.6 us -> 56.5 us
    pallas_call x1, Pallas kernels: 56.3 us -> 55.2 us  [on_device(): pl.pallas_call(functools.partial(main_kernel, n, mems, (columns, own, tgt...]
where the time goes in v8:
time: 57.3 us; the launch traced here: 57.1 us
  Pallas kernels  56.5 us (99%)
  between operations  0.64 us (1%)
    pallas_call x1, Pallas kernels, on_device(): pl.pallas_call(functools.partial(main_kernel, n, mems, (columns, own, tgt...  55.2 us
    pallas_call x1, Pallas kernels, on_device(): pl.pallas_call(functools.partial(last_kernel, (columns, members, fields,...  1.29 us

profile of v8, /device:TPU:96, one launch (start us, length us, event | category | flops | bytes accessed | tf_op | source)
XLA Modules:
  0.0 57.1 jit_solution(8258516218045471348)
XLA Ops:
  0.6 55.2 %regrid.1 = (f32[64,4096]{1,0:T(8,128)S(1)}, f32[1,384]{1,0:T(1,128)S(1)}) custom-call(bf16[64,16384]{1,0:T(8,128)(2,1)} %bitcast.8, f32[128,128]{1,0:T(8,128)} %bitcast.9, s32[128,128]{1,0:T(8,128)} %bitcast.10, f32[32,128]{1,0:T(8,128)} %bitcast.11, bf16[16,128,128]{2,1,0:T(8,128)(2,1)} %tiles_in.1, s32[24,32]{1,0:T(8,128)} %bitcast.12, ...), custom_call_target="tpu_custom_call" | custom-call | tf_op jit(solution)/shard_map/regrid/pallas_call | solution.py:531
  55.8 1.3 %finish.1 = (f32[64,4096]{1,0:T(8,128)}, f32[2,4,8]{2,1,0:T(4,128)}, f32[4,8]{1,0:T(4,128)}) custom-call(f32[1,384]{1,0:T(1,128)S(1)} %get-tuple-element.8.tot, f32[64,4096]{1,0:T(8,128)S(1)} %get-tuple-element.9.scaled), custom_call_target="tpu_custom_call" | custom-call | tf_op jit(solution)/shard_map/finish/pallas_call | solution.py:581

commit v9 on v8

--- a/solution.py
+++ b/solution.py
@@ -253,14 +253,14 @@
         s_msg[...] = s_msg[...] + rs0[...]
 
     others(send_lower, lambda m: (my_mem > m) & (me == 1))
-    pl.when(has_low)(to_up.wait_recv)
-    pl.when(has_up)(to_low.wait_recv)
 
     def send_higher(m):
         pl.semaphore_wait(mem_in.at[m], 1)
         from_mem(my_mem, m).start()
 
     others(send_higher, lambda m: my_mem < m)
+    pl.when(has_low)(to_up.wait_recv)
+    pl.when(has_up)(to_low.wait_recv)
 
     from_low = (lane >= tgt - reach) & has_low
     from_up = (lane < reach) & has_up
@@ -379,6 +379,34 @@
     for o in range(1, stride):
         pl.when((me > o) & is_first)(functools.partial(add_window, o))
 
+    def arrived(start, count, g):
+        at = rx.at[pl.ds(start, count)]
+        remote(at, at, dsend.at[0], drecv.at[g], {"band": lax.rem(me + 1, n)}).wait_recv()
+        for i in range(count):
+            mid[...] = mid[...] + rx[start + i]
+
+    def gather():
+        mine = lax.div(me, group)
+        near = jnp.where(via & (me == 0), 2, group - 1 - lax.rem(me, group))
+        mid[...] = jnp.zeros((1, WORDS), F32)
+        for count in range(1, group):
+            pl.when(is_first & (near == count))(functools.partial(arrived, me + 1, count, mine))
+
+        def add_group(g, carry):
+            arrived(group * g, group, g)
+            return carry
+
+        no_more = (via & (me == 0)) | jnp.logical_not(is_first)
+        lax.fori_loop(jnp.where(no_more, n // group, mine + 1), n // group, add_group, 0)
+
+    hands = via & (me == 1)
+    hand = remote(mid, rx.at[2], hsend, drecv.at[0], band(-1))
+
+    @pl.when(hands)
+    def _():
+        gather()
+        hand.start()
+
     def add_part(side, start):
         def body(j, carry):
             part_copy(1 - side, j).wait_recv()
@@ -427,27 +455,7 @@
         to_up.wait_send()
         parts_sent(1)
 
-    def arrived(start, count, g):
-        at = rx.at[pl.ds(start, count)]
-        remote(at, at, dsend.at[0], drecv.at[g], {"band": lax.rem(me + 1, n)}).wait_recv()
-        for i in range(count):
-            mid[...] = mid[...] + rx[start + i]
-
-    mine = lax.div(me, group)
-    near = jnp.where(via & (me == 0), 2, group - 1 - lax.rem(me, group))
-    mid[...] = jnp.zeros((1, WORDS), F32)
-    for count in range(1, group):
-        pl.when(is_first & (near == count))(functools.partial(arrived, me + 1, count, mine))
-
-    def add_group(g, carry):
-        arrived(group * g, group, g)
-        return carry
-
-    no_more = (via & (me == 0)) | jnp.logical_not(is_first)
-    lax.fori_loop(jnp.where(no_more, n // group, mine + 1), n // group, add_group, 0)
-
-    hand = remote(mid, rx.at[2], hsend, drecv.at[0], band(-1))
-    pl.when(via & (me == 1))(hand.start)
+    pl.when(jnp.logical_not(hands))(gather)
     run[...] = run[...] + mid[...]
 
     def total_to(p, words, to):
@@ -474,7 +482,7 @@
 
     for mine_to_give, count in gives:
         pl.when(mine_to_give)(total_to(me + 1, rx.at[0:count], rx.at[0:count]).wait_send)
-    pl.when(via & (me == 1))(hand.wait_send)
+    pl.when(hands)(hand.wait_send)
 
 
 def last_kernel(shape, mems, tot, scaled, out, conserved, ensemble, done, mean_v, group_v, sems):

time: 57.3 us -> 56.4 us (0.984)
  the two profiles are of different devices: /device:TPU:96 before, /device:TPU:224 now
where the time goes in v9:
time: 56.4 us; the launch traced here: 56.2 us
  Pallas kernels  55.6 us (99%)
  between operations  0.64 us (1%)
    pallas_call x1, Pallas kernels, on_device(): pl.pallas_call(functools.partial(main_kernel, n, mems, (columns, own, tgt...  54.3 us
    pallas_call x1, Pallas kernels, on_device(): pl.pallas_call(functools.partial(last_kernel, (columns, members, fields,...  1.29 us

profile of v9, /device:TPU:224, one launch (start us, length us, event | category | flops | bytes accessed | tf_op | source)
XLA Modules:
  0.0 56.2 jit_solution(15901310691400909885)
XLA Ops:
  0.6 54.3 %regrid.1 = (f32[64,4096]{1,0:T(8,128)S(1)}, f32[1,384]{1,0:T(1,128)S(1)}) custom-call(bf16[64,16384]{1,0:T(8,128)(2,1)} %bitcast.8, f32[128,128]{1,0:T(8,128)} %bitcast.9, s32[128,128]{1,0:T(8,128)} %bitcast.10, f32[32,128]{1,0:T(8,128)} %bitcast.11, bf16[16,128,128]{2,1,0:T(8,128)(2,1)} %tiles_in.1, s32[24,32]{1,0:T(8,128)} %bitcast.12, ...), custom_call_target="tpu_custom_call" | custom-call | tf_op jit(solution)/shard_map/regrid/pallas_call | solution.py:539
  54.9 1.3 %finish.1 = (f32[64,4096]{1,0:T(8,128)}, f32[2,4,8]{2,1,0:T(4,128)}, f32[4,8]{1,0:T(4,128)}) custom-call(f32[1,384]{1,0:T(1,128)S(1)} %get-tuple-element.8.tot, f32[64,4096]{1,0:T(8,128)S(1)} %get-tuple-element.9.scaled), custom_call_target="tpu_custom_call" | custom-call | tf_op jit(solution)/shard_map/finish/pallas_call | solution.py:589
